TPU v7x, 512 devices: a whole 4x4x16 slice. The times are simulated.
512 devices in a mesh: dp: 32 (over y, x, core), tp: 16 (over z).
Axes of the slice: x: 4, y: 4, z: 16, core: 2. Of those that a mesh axis runs over, the one named last changes fastest.
Arguments:
- slope_up: float32 [32, 1280, 5120], P('dp', None, 'tp'), may hold values from -1.25 to 1.25
- slope_down: float32 [32, 5120, 1280], P('dp', 'tp'), may hold values from -1.25 to 1.25
- slope_norm: float32 [32, 1280], P('dp'), may hold values from -12 to 12
- slope_bias: float32 [32, 1280], P('dp'), may hold values from -12 to 12
- param_up: float32 [1280, 5120], P('dp', 'tp'), may hold values from -0.15625 to 0.15625
- param_down: float32 [5120, 1280], P('tp', 'dp'), may hold values from -0.078125 to 0.078125
- param_norm: float32 [1280], P('dp'), may hold values from 0.25 to 1.75
- param_bias: float32 [1280], P('dp'), may hold values from -3 to 3
- state_up: float32 [1280, 5120], P('dp', 'tp'), may hold values from -1.75 to 1.75
- state_down: float32 [5120, 1280], P('tp', 'dp'), may hold values from -1.75 to 1.75
- state_norm: float32 [1280], P('dp'), may hold values from -1.75 to 1.75
- state_bias: float32 [1280], P('dp'), may hold values from -1.75 to 1.75
Outputs:
- half_up: bfloat16 [1280, 5120], P(None, 'tp')
- half_down: bfloat16 [5120, 1280], P('tp')
- half_norm: bfloat16 [1280], replicated
- half_bias: bfloat16 [1280], replicated
- next_up: float32 [1280, 5120], P('dp', 'tp')
- next_down: float32 [5120, 1280], P('tp', 'dp')
- next_norm: float32 [1280], P('dp')
- next_bias: float32 [1280], P('dp')
- state_new_up: float32 [1280, 5120], P('dp', 'tp')
- state_new_down: float32 [5120, 1280], P('tp', 'dp')
- state_new_norm: float32 [1280], P('dp')
- state_new_bias: float32 [1280], P('dp')
All inputs are finite; a program needn't handle non-finite values.
Results may differ from a plain program's by a relative error of at most 0.009.
Values may be sent and summed in bfloat16 or wider, within the bound.
No kernel may reach another device: no remote copies, remote signals or barrier semaphores. Data moves between devices by JAX's collectives and lax.ppermute only.
A program may use at most 64 MiB of HBM per device.

v0:
```python
import jax
import jax.numpy as jnp
from jax import lax
from jax.sharding import Mesh
from jax.sharding import PartitionSpec as P

DP = ("dp_0", "dp_1", "dp_2")


learn_rate = 0.1
hold_rate = 0.7


def split_up(shard, dim, length):
    lengths = shard.shape
    blocks = shard.reshape(*lengths[:dim], length, lengths[dim] // length, *lengths[dim + 1 :])
    return jnp.moveaxis(blocks, dim, 0)


def sent_and_summed(shard, axis, dim):
    length = lax.axis_size(axis)
    blocks = lax.all_to_all(split_up(shard, dim, length), axis, 0, 0, tiled=True)
    return jnp.sum(blocks.astype(jnp.float32), axis=0)


def sent_to_all(shard, axis):
    copies = jnp.broadcast_to(shard, (lax.axis_size(axis), *shard.shape))
    return lax.all_to_all(copies, axis, split_axis=0, concat_axis=0, tiled=True)


def in_order(blocks, dim):
    blocks = jnp.moveaxis(blocks, 0, dim)
    lengths = blocks.shape
    return blocks.reshape(*lengths[:dim], lengths[dim] * lengths[dim + 1], *lengths[dim + 2 :])


def whole_of(shard, axes, dim):
    far, near = axes
    blocks = sent_to_all(sent_to_all(shard, far), near)
    return in_order(blocks.swapaxes(0, 1).reshape(-1, *shard.shape), dim)


def body(
    slope_up,
    slope_down,
    slope_norm,
    slope_bias,
    param_up,
    param_down,
    param_norm,
    param_bias,
    state_up,
    state_down,
    state_norm,
    state_bias,
):
    mean_up, mean_down, mean_norm, mean_bias = (
        sent_and_summed(slope_up[0].astype(jnp.bfloat16), DP, 0),
        sent_and_summed(slope_down[0].astype(jnp.bfloat16), DP, 1),
        sent_and_summed(slope_norm[0].astype(jnp.bfloat16), DP, 0),
        sent_and_summed(slope_bias[0].astype(jnp.bfloat16), DP, 0),
    )
    mean_rate = lax.axis_size(DP) ** (-0.5)
    mean_up = mean_up * mean_rate
    mean_down = mean_down * mean_rate
    mean_norm = mean_norm * mean_rate
    mean_bias = mean_bias * mean_rate
    state_new_up = hold_rate * state_up + mean_up
    next_up = param_up - learn_rate * state_new_up
    state_new_down = hold_rate * state_down + mean_down
    next_down = param_down - learn_rate * state_new_down
    state_new_norm = hold_rate * state_norm + mean_norm
    next_norm = param_norm - learn_rate * state_new_norm
    state_new_bias = hold_rate * state_bias + mean_bias
    next_bias = param_bias - learn_rate * state_new_bias
    half_up, half_down, half_norm, half_bias = (
        whole_of(next_up.astype(jnp.bfloat16), (("dp_0", "dp_1"), "dp_2"), 0),
        whole_of(next_down.astype(jnp.bfloat16), (("dp_0", "dp_1"), "dp_2"), 1),
        whole_of(next_norm.astype(jnp.bfloat16), (("dp_0", "dp_1"), "dp_2"), 0),
        whole_of(next_bias.astype(jnp.bfloat16), (("dp_0", "dp_1"), "dp_2"), 0),
    )
    return (
        half_up,
        half_down,
        half_norm,
        half_bias,
        next_up,
        next_down,
        next_norm,
        next_bias,
        state_new_up,
        state_new_down,
        state_new_norm,
        state_new_bias,
    )


def solution(mesh):
    torus = Mesh(mesh.devices.reshape(4, 4, 2, mesh.shape["tp"]), ("dp_0", "dp_1", "dp_2", "tp"))
    placed = (
        P(DP, None, "tp"),
        P(DP, "tp", None),
        P(DP, None),
        P(DP, None),
        P(DP, "tp"),
        P("tp", DP),
        P(DP),
        P(DP),
        P(DP, "tp"),
        P("tp", DP),
        P(DP),
        P(DP),
    )
    return jax.shard_map(
        body,
        mesh=torus,
        in_specs=placed,
        out_specs=(
            P(None, "tp"),
            P("tp", None),
            P(),
            P(),
            P(DP, "tp"),
            P("tp", DP),
            P(DP),
            P(DP),
            P(DP, "tp"),
            P("tp", DP),
            P(DP),
            P(DP),
        ),
        check_vma=False,
    )
```

profile of v0, /device:TPU:1, one launch (start us, length us, event | category | flops | bytes accessed | tf_op | source)
XLA Modules:
  0.0 145.9 jit_solution(6584083236521728388)
XLA Ops:
  0.6 0.7 convert_reduce_fusion.5
  1.4 0.7 convert_element_type.84
  2.1 10.3 %all-to-all-start.6 = ((bf16[32,1,40]{2,1,0:T(2,128)(2,1)}), bf16[32,1,40]{2,1,0:T(2,128)(2,1)S(1)}, u32[]{:S(2)}, u32[]{:S(2)}) async-start(bf16[32,1,40]{2,1,0:T(2,128)(2,1)} %convert_element_type.84), calls=%async_computation.6 | async-start | bytes 32768 | tf_op jit(solution)/shard_map/all_to_all | solution.py:22
  12.4 0.7 convert_reduce_fusion.4
  13.8 5.6 %all-to-all-done.6 = bf16[32,1,40]{2,1,0:T(2,128)(2,1)S(1)} async-done(((bf16[32,1,40]{2,1,0:T(2,128)(2,1)}), bf16[32,1,40]{2,1,0:T(2,128)(2,1)S(1)}, u32[]{:S(2)}, u32[]{:S(2)}) %all-to-all-start.6) | async-done | bytes 2592 | tf_op jit(solution)/shard_map/all_to_all | solution.py:22
  19.4 4.1 %all-to-all-start.9 = ((bf16[32,1,40]{2,1,0:T(2,128)(2,1)}), bf16[32,1,40]{2,1,0:T(2,128)(2,1)S(1)}, u32[]{:S(2)}, u32[]{:S(2)}) async-start(bf16[32,1,40]{2,1,0:T(2,128)(2,1)} %convert_element_type.85), calls=%async_computation.9 | async-start | bytes 32768 | tf_op jit(solution)/shard_map/all_to_all | solution.py:22
  23.6 1.2 fusion.1
  24.8 5.8 %all-to-all-done.9 = bf16[32,1,40]{2,1,0:T(2,128)(2,1)S(1)} async-done(((bf16[32,1,40]{2,1,0:T(2,128)(2,1)}), bf16[32,1,40]{2,1,0:T(2,128)(2,1)S(1)}, u32[]{:S(2)}, u32[]{:S(2)}) %all-to-all-start.9) | async-done | bytes 2592 | tf_op jit(solution)/shard_map/all_to_all | solution.py:22
  31.1 3.5 %all-to-all-start.7 = ((bf16[16,1,40]{2,1,0:T(2,128)(2,1)}), bf16[16,1,40]{2,1,0:T(2,128)(2,1)S(1)}, u32[]{:S(2)}, u32[]{:S(2)}) async-start(bf16[16,1,40]{2,1,0:T(2,128)(2,1)} %broadcast_in_dim.28), calls=%async_computation.7 | async-start | bytes 16384 | tf_op jit(solution)/shard_map/all_to_all | solution.py:28
  34.7 1.2 fusion
  35.9 5.1 %all-to-all-done.7 = bf16[16,1,40]{2,1,0:T(2,128)(2,1)S(1)} async-done(((bf16[16,1,40]{2,1,0:T(2,128)(2,1)}), bf16[16,1,40]{2,1,0:T(2,128)(2,1)S(1)}, u32[]{:S(2)}, u32[]{:S(2)}) %all-to-all-start.7) | async-done | bytes 1312 | tf_op jit(solution)/shard_map/all_to_all | solution.py:28
  41.5 3.5 %all-to-all-start.10 = ((bf16[16,1,40]{2,1,0:T(2,128)(2,1)}), bf16[16,1,40]{2,1,0:T(2,128)(2,1)S(1)}, u32[]{:S(2)}, u32[]{:S(2)}) async-start(bf16[16,1,40]{2,1,0:T(2,128)(2,1)} %broadcast_in_dim.30), calls=%async_computation.10 | async-start | bytes 16384 | tf_op jit(solution)/shard_map/all_to_all | solution.py:28
  45.0 2.4 %copy.37 = bf16[1,1280,320]{2,1,0:T(8,128)(2,1)} copy(f32[1,1280,320]{1,2,0:T(8,128)} %param.12) | data formatting | bytes 2457600 | tf_op args[0]
  48.1 3.2 %all-to-all-done.10 = bf16[16,1,40]{2,1,0:T(2,128)(2,1)S(1)} async-done(((bf16[16,1,40]{2,1,0:T(2,128)(2,1)}), bf16[16,1,40]{2,1,0:T(2,128)(2,1)S(1)}, u32[]{:S(2)}, u32[]{:S(2)}) %all-to-all-start.10) | async-done | bytes 1312 | tf_op jit(solution)/shard_map/all_to_all | solution.py:28
  51.3 6.2 %all-to-all-start.8 = ((bf16[2,2,320]{2,1,0:T(2,128)(2,1)}), bf16[2,2,320]{2,1,0:T(2,128)(2,1)S(1)}, u32[]{:S(2)}, u32[]{:S(2)}) async-start(bf16[2,2,320]{2,1,0:T(2,128)(2,1)} %reshape.80), calls=%async_computation.8 | async-start | bytes 6144 | tf_op jit(solution)/shard_map/all_to_all | solution.py:28
  57.6 0.9 all-to-all-done.8
  58.5 3.7 %all_to_all.70 = bf16[2,2,320]{2,1,0:T(2,128)(2,1)S(1)} all-to-all(bf16[2,2,320]{2,1,0:T(2,128)(2,1)S(1)} %reshape.82), channel_id=1, replica_groups=mesh['dp_0'=4,'dp_1'=4,'dp_2'=2,'tp'=16] {'dp_2'}, dimensions={0} | all-to-all | bytes 5120 | tf_op jit(solution)/shard_map/all_to_all | solution.py:28
  62.2 3.9 %all-to-all-start = ((bf16[32,40,320]{2,1,0:T(8,128)(2,1)}), bf16[32,40,320]{2,1,0:T(8,128)(2,1)S(1)}, u32[]{:S(2)}, u32[]{:S(2)}) async-start(bf16[32,40,320]{2,1,0:T(8,128)(2,1)} %bitcast), calls=%async_computation | async-start | bytes 1966080 | tf_op jit(solution)/shard_map/all_to_all | solution.py:22
  66.1 2.4 %copy.39 = bf16[1,320,1280]{1,2,0:T(8,128)(2,1)} copy(f32[1,320,1280]{2,1,0:T(8,128)} %param.13) | data formatting | bytes 2457600 | tf_op args[1]
  68.5 14.0 %all-to-all-done = bf16[32,40,320]{2,1,0:T(8,128)(2,1)S(1)} async-done(((bf16[32,40,320]{2,1,0:T(8,128)(2,1)}), bf16[32,40,320]{2,1,0:T(8,128)(2,1)S(1)}, u32[]{:S(2)}, u32[]{:S(2)}) %all-to-all-start) | async-done | bytes 819232 | tf_op jit(solution)/shard_map/all_to_all | solution.py:22
  82.6 4.0 %all-to-all-start.3 = ((bf16[32,320,40]{1,2,0:T(8,128)(2,1)}), bf16[32,320,40]{1,2,0:T(8,128)(2,1)S(1)}, u32[]{:S(2)}, u32[]{:S(2)}) async-start(bf16[32,320,40]{1,2,0:T(8,128)(2,1)} %bitcast.4), calls=%async_computation.3 | async-start | bytes 1966080 | tf_op jit(solution)/shard_map/all_to_all | solution.py:22
  87.4 15.6 %all-to-all-done.3 = bf16[32,320,40]{1,2,0:T(8,128)(2,1)S(1)} async-done(((bf16[32,320,40]{1,2,0:T(8,128)(2,1)}), bf16[32,320,40]{1,2,0:T(8,128)(2,1)S(1)}, u32[]{:S(2)}, u32[]{:S(2)}) %all-to-all-start.3) | async-done | bytes 819232 | tf_op jit(solution)/shard_map/all_to_all | solution.py:22
  103.0 0.8 broadcast_in_dim.24
  103.8 3.6 %all-to-all-start.1 = ((bf16[16,40,320]{2,1,0:T(8,128)(2,1)}), bf16[16,40,320]{2,1,0:T(8,128)(2,1)S(1)}, u32[]{:S(2)}, u32[]{:S(2)}) async-start(bf16[16,40,320]{2,1,0:T(8,128)(2,1)} %broadcast_in_dim.24), calls=%async_computation.1 | async-start | bytes 983040 | tf_op jit(solution)/shard_map/all_to_all | solution.py:28
  108.3 9.7 %all-to-all-done.1 = bf16[16,40,320]{2,1,0:T(8,128)(2,1)S(1)} async-done(((bf16[16,40,320]{2,1,0:T(8,128)(2,1)}), bf16[16,40,320]{2,1,0:T(8,128)(2,1)S(1)}, u32[]{:S(2)}, u32[]{:S(2)}) %all-to-all-start.1) | async-done | bytes 409632 | tf_op jit(solution)/shard_map/all_to_all | solution.py:28
  118.0 5.7 %all_to_all.71 = bf16[2,16,40,320]{3,2,1,0:T(8,128)(2,1)S(1)} all-to-all(bf16[2,16,40,320]{3,2,1,0:T(8,128)(2,1)S(1)} %broadcast_in_dim.25), channel_id=1, replica_groups=mesh['dp_0'=4,'dp_1'=4,'dp_2'=2,'tp'=16] {'dp_2'}, dimensions={0} | all-to-all | bytes 1638400 | tf_op jit(solution)/shard_map/all_to_all | solution.py:28
  123.7 0.8 broadcast_in_dim.26
  124.6 3.6 %all-to-all-start.4 = ((bf16[16,320,40]{1,2,0:T(8,128)(2,1)}), bf16[16,320,40]{1,2,0:T(8,128)(2,1)S(1)}, u32[]{:S(2)}, u32[]{:S(2)}) async-start(bf16[16,320,40]{1,2,0:T(8,128)(2,1)} %broadcast_in_dim.26), calls=%async_computation.4 | async-start | bytes 983040 | tf_op jit(solution)/shard_map/all_to_all | solution.py:28
  129.8 1.3 copy.45
  131.1 7.6 %all-to-all-done.4 = bf16[16,320,40]{1,2,0:T(8,128)(2,1)S(1)} async-done(((bf16[16,320,40]{1,2,0:T(8,128)(2,1)}), bf16[16,320,40]{1,2,0:T(8,128)(2,1)S(1)}, u32[]{:S(2)}, u32[]{:S(2)}) %all-to-all-start.4) | async-done | bytes 409632 | tf_op jit(solution)/shard_map/all_to_all | solution.py:28
  138.8 5.7 %all_to_all.72 = bf16[2,16,320,40]{2,3,1,0:T(8,128)(2,1)S(1)} all-to-all(bf16[2,16,320,40]{2,3,1,0:T(8,128)(2,1)S(1)} %broadcast_in_dim.27), channel_id=1, replica_groups=mesh['dp_0'=4,'dp_1'=4,'dp_2'=2,'tp'=16] {'dp_2'}, dimensions={0} | all-to-all | bytes 1638400 | tf_op jit(solution)/shard_map/all_to_all | solution.py:28
  144.6 1.3 copy.46
  (33 shorter events, 6.4 us)
Async XLA Ops:
  2.1 17.3 %all-to-all-start.6 = ((bf16[32,1,40]{2,1,0:T(2,128)(2,1)}), bf16[32,1,40]{2,1,0:T(2,128)(2,1)S(1)}, u32[]{:S(2)}, u32[]{:S(2)}) async-start(bf16[32,1,40]{2,1,0:T(2,128)(2,1)} %convert_element_type.84), calls=%async_computation.6 | async-start | bytes 32768 | tf_op jit(solution)/shard_map/all_to_all | solution.py:22
  19.4 11.1 %all-to-all-start.9 = ((bf16[32,1,40]{2,1,0:T(2,128)(2,1)}), bf16[32,1,40]{2,1,0:T(2,128)(2,1)S(1)}, u32[]{:S(2)}, u32[]{:S(2)}) async-start(bf16[32,1,40]{2,1,0:T(2,128)(2,1)} %convert_element_type.85), calls=%async_computation.9 | async-start | bytes 32768 | tf_op jit(solution)/shard_map/all_to_all | solution.py:22
  31.1 9.8 %all-to-all-start.7 = ((bf16[16,1,40]{2,1,0:T(2,128)(2,1)}), bf16[16,1,40]{2,1,0:T(2,128)(2,1)S(1)}, u32[]{:S(2)}, u32[]{:S(2)}) async-start(bf16[16,1,40]{2,1,0:T(2,128)(2,1)} %broadcast_in_dim.28), calls=%async_computation.7 | async-start | bytes 16384 | tf_op jit(solution)/shard_map/all_to_all | solution.py:28
  41.5 9.8 %all-to-all-start.10 = ((bf16[16,1,40]{2,1,0:T(2,128)(2,1)}), bf16[16,1,40]{2,1,0:T(2,128)(2,1)S(1)}, u32[]{:S(2)}, u32[]{:S(2)}) async-start(bf16[16,1,40]{2,1,0:T(2,128)(2,1)} %broadcast_in_dim.30), calls=%async_computation.10 | async-start | bytes 16384 | tf_op jit(solution)/shard_map/all_to_all | solution.py:28
  51.3 7.2 %all-to-all-start.8 = ((bf16[2,2,320]{2,1,0:T(2,128)(2,1)}), bf16[2,2,320]{2,1,0:T(2,128)(2,1)S(1)}, u32[]{:S(2)}, u32[]{:S(2)}) async-start(bf16[2,2,320]{2,1,0:T(2,128)(2,1)} %reshape.80), calls=%async_computation.8 | async-start | bytes 6144 | tf_op jit(solution)/shard_map/all_to_all | solution.py:28
  62.2 20.4 %all-to-all-start = ((bf16[32,40,320]{2,1,0:T(8,128)(2,1)}), bf16[32,40,320]{2,1,0:T(8,128)(2,1)S(1)}, u32[]{:S(2)}, u32[]{:S(2)}) async-start(bf16[32,40,320]{2,1,0:T(8,128)(2,1)} %bitcast), calls=%async_computation | async-start | bytes 1966080 | tf_op jit(solution)/shard_map/all_to_all | solution.py:22
  68.5 18.2 %copy-start = (f32[40,320]{1,0:T(8,128)S(1)}, f32[40,320]{1,0:T(8,128)}, u32[]{:S(2)}) copy-start(f32[40,320]{1,0:T(8,128)} %param.16) | copy-start | bytes 153604
  68.5 18.2 %copy-start.1 = (f32[40,320]{1,0:T(8,128)S(1)}, f32[40,320]{1,0:T(8,128)}, u32[]{:S(2)}) copy-start(f32[40,320]{1,0:T(8,128)} %param.20) | copy-start | bytes 153604
  82.6 20.4 %all-to-all-start.3 = ((bf16[32,320,40]{1,2,0:T(8,128)(2,1)}), bf16[32,320,40]{1,2,0:T(8,128)(2,1)S(1)}, u32[]{:S(2)}, u32[]{:S(2)}) async-start(bf16[32,320,40]{1,2,0:T(8,128)(2,1)} %bitcast.4), calls=%async_computation.3 | async-start | bytes 1966080 | tf_op jit(solution)/shard_map/all_to_all | solution.py:22
  86.7 20.8 %copy-start.2 = (f32[320,40]{0,1:T(8,128)S(1)}, f32[320,40]{0,1:T(8,128)}, u32[]{:S(2)}) copy-start(f32[320,40]{0,1:T(8,128)} %param.17) | copy-start | bytes 153604
  86.7 20.8 %copy-start.3 = (f32[320,40]{0,1:T(8,128)S(1)}, f32[320,40]{0,1:T(8,128)}, u32[]{:S(2)}) copy-start(f32[320,40]{0,1:T(8,128)} %param.21) | copy-start | bytes 153604
  103.8 14.1 %all-to-all-start.1 = ((bf16[16,40,320]{2,1,0:T(8,128)(2,1)}), bf16[16,40,320]{2,1,0:T(8,128)(2,1)S(1)}, u32[]{:S(2)}, u32[]{:S(2)}) async-start(bf16[16,40,320]{2,1,0:T(8,128)(2,1)} %broadcast_in_dim.24), calls=%async_computation.1 | async-start | bytes 983040 | tf_op jit(solution)/shard_map/all_to_all | solution.py:28
  124.6 14.2 %all-to-all-start.4 = ((bf16[16,320,40]{1,2,0:T(8,128)(2,1)}), bf16[16,320,40]{1,2,0:T(8,128)(2,1)S(1)}, u32[]{:S(2)}, u32[]{:S(2)}) async-start(bf16[16,320,40]{1,2,0:T(8,128)(2,1)} %broadcast_in_dim.26), calls=%async_computation.4 | async-start | bytes 983040 | tf_op jit(solution)/shard_map/all_to_all | solution.py:28
where the time goes:
time: 147 us; the launch traced here: 146 us
  waiting for transfers between devices  67.5 us (46%)
  starting transfers between devices  42.6 us (29%)
  blocking collectives  15.1 us (10%)
  local copies, waits for them, and re-layouts  14.3 us (10%)
  other arithmetic  5.57 us (4%)
    all_to_all x4, waiting for transfers between devices, sent_and_summed(): lax.all_to_all(split_up(shard, dim, length), axis, 0, 0, tiled=True)  41 us
    all_to_all x5, waiting for transfers between devices, sent_to_all(): return lax.all_to_all(copies, axis, split_axis=0, concat_axis=0, tiled=True)  26.5 us
    all_to_all x4, starting transfers between devices, sent_and_summed(): lax.all_to_all(split_up(shard, dim, length), axis, 0, 0, tiled=True)  22.3 us
    all_to_all x5, starting transfers between devices, sent_to_all(): return lax.all_to_all(copies, axis, split_axis=0, concat_axis=0, tiled=True)  20.2 us
    all_to_all x3, blocking collectives, sent_to_all(): return lax.all_to_all(copies, axis, split_axis=0, concat_axis=0, tiled=True)  15.1 us
    unnamed x18, local copies, waits for them, and re-layouts  8.3 us
    broadcast_in_dim x8, local copies, waits for them, and re-layouts, sent_to_all(): copies = jnp.broadcast_to(shard, (lax.axis_size(axis), *shard.shape))  3.03 us
  transfers between devices with their start and end apart: 9, of which 9 were waited for; matrix products, arithmetic and copies ran while one was open for 10% of the time, Pallas kernels for 0%

commit v1 on v0

v1 whole, which is shorter than its diff:
```python
import functools

import jax
import jax.numpy as jnp
from jax import lax
from jax.experimental import pallas as pl
from jax.experimental.pallas import tpu as pltpu
from jax.sharding import Mesh
from jax.sharding import PartitionSpec as P

DP = ("dp_0", "dp_1", "dp_2")
CHIPS = ("dp_0", "dp_1")
CORE = "dp_2"

learn_rate = 0.1
hold_rate = 0.7

SHARE = 40
COLS = 320
FOLD = 24
ROWS = 2 * SHARE + FOLD
HALF = 64


def eye(rows, cols, period=None):
    row = lax.broadcasted_iota(jnp.int32, (rows, cols), 0)
    col = lax.broadcasted_iota(jnp.int32, (rows, cols), 1)
    same = row == col
    if period:
        same = same | (row + period == col)
    return same.astype(jnp.bfloat16)


def times_transposed(a, b):
    return lax.dot_general(a, b, (((1,), (1,)), ((), ())), preferred_element_type=jnp.float32)


def low_lanes(rows):
    return lax.broadcasted_iota(jnp.int32, (rows, 128), 1) < HALF


def packed(first, second, tail, corner):
    upper = jnp.concatenate([tail[FOLD:], corner], axis=0)
    return jnp.concatenate([first, second, jnp.where(low_lanes(FOLD), tail[:FOLD], upper)], axis=0)


def split_kernel(chips, small, core_ref, x_ref, *refs):
    if small:
        norm_ref, bias_ref, keep_ref, send_ref = refs
    else:
        keep_ref, send_ref = refs
    first_core = core_ref[0] == 0
    one = eye(128, 128)
    blocks = []
    for k in range(chips * 2 * SHARE // 128):
        x = x_ref[:, k * 128 : (k + 1) * 128].astype(jnp.bfloat16)
        tail = x[256:]
        blocks.append(
            [
                times_transposed(one, x[:128]),
                times_transposed(one, x[128:256]),
                times_transposed(one, jnp.concatenate([tail, tail], axis=0)),
            ]
        )
    first, second, tail = (jnp.concatenate([b[j] for b in blocks], axis=0) for j in range(3))
    if small:
        zeros = jnp.zeros((1, HALF), jnp.float32)
        line = [jnp.concatenate([zeros, ref[...], zeros], axis=1) for ref in (norm_ref, bias_ref)]
        lines = jnp.concatenate(line + [jnp.zeros((6, line[0].shape[1]), jnp.float32)], axis=0)
    for i in range(chips):
        pair = []
        for c in range(2):
            at = (2 * i + c) * SHARE
            corner = lines[:, at : at + 128] if small else jnp.zeros((8, 128), jnp.float32)
            rows = slice(at, at + SHARE)
            pair.append(packed(first[rows], second[rows], tail[rows], corner))
        keep_ref[i] = jnp.where(first_core, pair[0], pair[1]).astype(jnp.bfloat16)
        send_ref[i] = jnp.where(first_core, pair[1], pair[0]).astype(jnp.bfloat16)


def split(core, x, small=()):
    cols, width = x.shape
    chips = width // (2 * SHARE)
    steps = 1 if small else 2
    out = jax.ShapeDtypeStruct((chips, ROWS, 128), jnp.bfloat16)
    spec = pl.BlockSpec((chips // steps, ROWS, 128), lambda i: (i, 0, 0))
    return pl.pallas_call(
        functools.partial(split_kernel, chips // steps, bool(small)),
        grid=(steps,),
        in_specs=[
            pl.BlockSpec(memory_space=pltpu.SMEM),
            pl.BlockSpec((cols, width // steps), lambda i: (0, i)),
        ]
        + [pl.BlockSpec((1, width), lambda i: (0, 0)) for _ in small],
        out_specs=[spec, spec],
        out_shape=[out, out],
    )(core, x, *small)


def moved(total, state, param, rate):
    state_new = hold_rate * state + total * rate
    return state_new, param - learn_rate * state_new


def update_kernel(rate, small, got_ref, param_ref, state_ref, *refs):
    if small:
        small_param_ref, small_state_ref, half_ref, next_ref, new_ref, small_next_ref, small_new_ref = refs
    else:
        half_ref, next_ref, new_ref = refs
    total = jnp.sum(got_ref[...].astype(jnp.float32), axis=0)
    folded = total[2 * SHARE :]
    shifted = jnp.concatenate([folded[:, HALF:], folded[:, :HALF]], axis=1)
    tail = jnp.concatenate([folded[:FOLD, :HALF], shifted[: SHARE - FOLD, :HALF]], axis=0)
    mean = jnp.concatenate([total[:SHARE], total[SHARE : 2 * SHARE], tail], axis=1)
    new, nxt = moved(mean, state_ref[...], param_ref[...], rate)
    new_ref[...] = new
    next_ref[...] = nxt
    if small:
        small_new, small_next = moved(folded[SHARE - FOLD :], small_state_ref[...], small_param_ref[...], rate)
        small_new_ref[...] = small_new
        small_next_ref[...] = small_next
        corner = small_next
    else:
        corner = jnp.zeros((8, 128), jnp.float32)
    twice = jnp.concatenate([nxt[:, 256:], nxt[:, 256:]], axis=1)
    half = packed(nxt[:, :128], nxt[:, 128:256], twice, corner).astype(jnp.bfloat16)
    for i in range(half_ref.shape[0]):
        half_ref[i] = half


def update(rate, got, param, state, small=()):
    mat = jax.ShapeDtypeStruct(param.shape, jnp.float32)
    line = jax.ShapeDtypeStruct((8, 128), jnp.float32)
    return pl.pallas_call(
        functools.partial(update_kernel, rate, bool(small)),
        out_shape=[jax.ShapeDtypeStruct(got.shape, jnp.bfloat16), mat, mat] + [line, line] * bool(small),
    )(got, param, state, *small)


def join_kernel(chips, core_ref, mine_ref, other_ref, out_ref):
    first_core = core_ref[0] == 0
    low = low_lanes(FOLD)
    parts = [[], [], []]
    for i in range(chips):
        mine = mine_ref[i].astype(jnp.float32)
        other = other_ref[i].astype(jnp.float32)
        for block in (jnp.where(first_core, mine, other), jnp.where(first_core, other, mine)):
            tail = block[2 * SHARE :]
            upper = SHARE - FOLD
            parts[0].append(block[:SHARE])
            parts[1].append(block[SHARE : 2 * SHARE])
            parts[2].append(jnp.where(low, tail, 0.0))
            parts[2].append(jnp.where(low[:upper], 0.0, tail[:upper]))
    first, second, tail = (jnp.concatenate(p, axis=0).astype(jnp.bfloat16) for p in parts)
    one = eye(128, 128)
    out_ref[:128] = times_transposed(one, first).astype(jnp.bfloat16)
    out_ref[128:256] = times_transposed(one, second).astype(jnp.bfloat16)
    out_ref[256:] = times_transposed(eye(HALF, 128, HALF), tail).astype(jnp.bfloat16)


def join(core, mine, other):
    chips = mine.shape[0]
    width = chips * 2 * SHARE
    steps = 2
    spec = pl.BlockSpec((chips // steps, ROWS, 128), lambda i: (i, 0, 0))
    return pl.pallas_call(
        functools.partial(join_kernel, chips // steps),
        grid=(steps,),
        in_specs=[pl.BlockSpec(memory_space=pltpu.SMEM), spec, spec],
        out_specs=pl.BlockSpec((COLS, width // steps), lambda i: (0, i)),
        out_shape=jax.ShapeDtypeStruct((COLS, width), jnp.bfloat16),
    )(core, mine, other)


def swapped(x):
    return lax.ppermute(x, CORE, [(0, 1), (1, 0)])


def over_chips(x):
    return lax.all_to_all(x, CHIPS, 0, 0, tiled=True)


def lines_of(first, second):
    return jnp.pad(jnp.stack([first, second]), ((0, 6), (HALF, HALF - first.shape[0])))


def body(
    slope_up,
    slope_down,
    slope_norm,
    slope_bias,
    param_up,
    param_down,
    param_norm,
    param_bias,
    state_up,
    state_down,
    state_norm,
    state_bias,
):
    rate = lax.axis_size(DP) ** (-0.5)
    core = lax.axis_index(CORE).astype(jnp.int32).reshape(1)

    keep_down, send_down = split(core, slope_down[0], (slope_norm, slope_bias))
    keep_up, send_up = split(core, slope_up[0].T)
    sum_down = keep_down + swapped(send_down)
    sum_up = keep_up + swapped(send_up)
    got_down = over_chips(sum_down)
    got_up = over_chips(sum_up)
    small = (lines_of(param_norm, param_bias), lines_of(state_norm, state_bias))
    copies_down, next_down, new_down, next_lines, new_lines = update(
        rate, got_down, param_down.T, state_down.T, small
    )
    copies_up, next_up, new_up = update(rate, got_up, param_up, state_up)
    mine_down = over_chips(copies_down)
    mine_up = over_chips(copies_up)
    other_down = swapped(mine_down)
    other_up = swapped(mine_up)
    half_down = join(core, mine_down, other_down)
    half_up = join(core, mine_up, other_up).T

    def corner(blocks):
        return blocks[:, ROWS - 8 : ROWS - 6, HALF : HALF + SHARE]

    is_first = core[0] == 0
    mine, other = corner(mine_down), corner(other_down)
    zero, one = jnp.where(is_first, mine, other), jnp.where(is_first, other, mine)
    halves = jnp.stack([zero, one], axis=1)
    half_norm = halves[:, :, 0].reshape(-1)
    half_bias = halves[:, :, 1].reshape(-1)

    def line(lines, row):
        return lines[row, HALF : HALF + SHARE]

    return (
        half_up,
        half_down,
        half_norm,
        half_bias,
        next_up,
        next_down.T,
        line(next_lines, 0),
        line(next_lines, 1),
        new_up,
        new_down.T,
        line(new_lines, 0),
        line(new_lines, 1),
    )


def solution(mesh):
    torus = Mesh(mesh.devices.reshape(4, 4, 2, mesh.shape["tp"]), ("dp_0", "dp_1", "dp_2", "tp"))
    placed = (
        P(DP, None, "tp"),
        P(DP, "tp", None),
        P(DP, None),
        P(DP, None),
        P(DP, "tp"),
        P("tp", DP),
        P(DP),
        P(DP),
        P(DP, "tp"),
        P("tp", DP),
        P(DP),
        P(DP),
    )
    return jax.shard_map(
        body,
        mesh=torus,
        in_specs=placed,
        out_specs=(
            P(None, "tp"),
            P("tp", None),
            P(),
            P(),
            P(DP, "tp"),
            P("tp", DP),
            P(DP),
            P(DP),
            P(DP, "tp"),
            P("tp", DP),
            P(DP),
            P(DP),
        ),
        check_vma=False,
    )
```

time: 147 us -> 84.4 us (0.57)
  waiting for transfers between devices: 67.5 us -> 23.4 us
  blocking collectives: 15.1 us -> 0 us
  Pallas kernels: 0 us -> 15 us
  local copies, waits for them, and re-layouts: 14.3 us -> 3.57 us
  starting transfers between devices: 42.6 us -> 37.5 us
  other arithmetic: 5.57 us -> 3.22 us
    all_to_all x9 -> x4, waiting for transfers between devices: 67.5 us -> 23.4 us  [over_chips(): return lax.all_to_all(x, CHIPS, 0, 0, tiled=True)]
    all_to_all x9 -> x4, starting transfers between devices: 42.6 us -> 14.4 us  [over_chips(): return lax.all_to_all(x, CHIPS, 0, 0, tiled=True)]
    ppermute x0 -> x4, starting transfers between devices: none -> 23.2 us  [swapped(): return lax.ppermute(x, CORE, [(0, 1), (1, 0)])]
    all_to_all x3 -> x0, blocking collectives: 15.1 us -> none  [sent_to_all(): return lax.all_to_all(copies, axis, split_axis=0, concat_axis=0, tiled=True)]
    pallas_call x0 -> x6, Pallas kernels: none -> 15 us  [the longest x2 6.05 us: split(): pl.pallas_call(functools.partial(split_kernel, chips // steps, bool(small...]
    unnamed x18 -> x24, local copies, waits for them, and re-layouts: 8.3 us -> 0.81 us
    convert_element_type x6 -> x0, other arithmetic: 5.14 us -> none  [the longest x1 1.19 us: body(): next_norm.astype(jnp.bfloat16)]
    broadcast_in_dim x8 -> x0, local copies, waits for them, and re-layouts: 3.03 us -> none  [sent_to_all(): copies = jnp.broadcast_to(shard, (lax.axis_size(axis), *shard.shape))]
  transfers between devices with their start and end apart: 9 -> 8, of which waited for: 9 -> 4; matrix products, arithmetic and copies ran while one was open for 10% -> 7% of each run, Pallas kernels for 0% -> 11%
where the time goes in v1:
time: 84.4 us; the launch traced here: 83.6 us
  starting transfers between devices  37.5 us (44%)
  waiting for transfers between devices  23.4 us (28%)
  Pallas kernels  15 us (18%)
  local copies, waits for them, and re-layouts  3.57 us (4%)
  other arithmetic  3.22 us (4%)
    all_to_all x4, waiting for transfers between devices, over_chips(): return lax.all_to_all(x, CHIPS, 0, 0, tiled=True)  23.4 us
    ppermute x4, starting transfers between devices, swapped(): return lax.ppermute(x, CORE, [(0, 1), (1, 0)])  23.2 us
    all_to_all x4, starting transfers between devices, over_chips(): return lax.all_to_all(x, CHIPS, 0, 0, tiled=True)  14.4 us
    pallas_call x2, Pallas kernels, split(): pl.pallas_call(functools.partial(split_kernel, chips // steps, bool(small...  6.05 us
    pallas_call x2, Pallas kernels, join(): pl.pallas_call(functools.partial(join_kernel, chips // steps), grid=(step...  4.9 us
    pallas_call x2, Pallas kernels, update(): pl.pallas_call(functools.partial(update_kernel, rate, bool(small)), out_s...  4.05 us
  transfers between devices with their start and end apart: 8, of which 4 were waited for; matrix products, arithmetic and copies ran while one was open for 7% of the time, Pallas kernels for 11%

profile of v1, /device:TPU:1, one launch (start us, length us, event | category | flops | bytes accessed | tf_op | source)
XLA Modules:
  0.0 83.6 jit_solution(18106695555244993195)
XLA Ops:
  0.6 3.2 %shard_map.214 = (bf16[16,104,128]{2,1,0:T(8,128)(2,1)}, bf16[16,104,128]{2,1,0:T(8,128)(2,1)}) custom-call(s32[1]{0:T(128)} %bitcast.core_ref, f32[320,1280]{1,0:T(8,128)} %bitcast.30, f32[1,1280]{1,0:T(1,128)} %refs_0_.1, f32[1,1280]{1,0:T(1,128)} %refs_1_.1), custom_call_target="tpu_custom_call" | custom-call | tf_op jit(solution)/shard_map/pallas_call | solution.py:87
  3.8 8.9 %collective-permute-start.2 = (bf16[16,104,128]{2,1,0:T(8,128)(2,1)}, bf16[16,104,128]{2,1,0:T(8,128)(2,1)S(1)}, u32[]{:S(2)}, u32[]{:S(2)}) collective-permute-start(bf16[16,104,128]{2,1,0:T(8,128)(2,1)} %get-tuple-element.28), channel_id=1, source_target_pairs={{0,16},{16,0},{1,17},{17,1},{2,18},{18,2},{3,19},{19,3},{4,20},{20... | collective-permute-start | bytes 1277960 | tf_op jit(solution)/shard_map/ppermute | solution.py:176
  12.7 2.9 %shard_map.211 = (bf16[16,104,128]{2,1,0:T(8,128)(2,1)}, bf16[16,104,128]{2,1,0:T(8,128)(2,1)}) custom-call(s32[1]{0:T(128)} %bitcast.core_ref, f32[320,1280]{1,0:T(8,128)} %bitcast.31), custom_call_target="tpu_custom_call" | custom-call | tf_op jit(solution)/shard_map/pallas_call | solution.py:87
  15.6 2.0 %collective-permute-start = (bf16[16,104,128]{2,1,0:T(8,128)(2,1)}, bf16[16,104,128]{2,1,0:T(8,128)(2,1)S(1)}, u32[]{:S(2)}, u32[]{:S(2)}) collective-permute-start(bf16[16,104,128]{2,1,0:T(8,128)(2,1)} %get-tuple-element.25), channel_id=1, source_target_pairs={{0,16},{16,0},{1,17},{17,1},{2,18},{18,2},{3,19},{19,3},{4,20},{20... | collective-permute-start | bytes 1277960 | tf_op jit(solution)/shard_map/ppermute | solution.py:176
  17.6 0.0 collective-permute-done.2
  17.6 0.0 copy-done.6
  17.6 0.9 %add.11 = bf16[16,104,128]{2,1,0:T(8,128)(2,1)} add(bf16[16,104,128]{2,1,0:T(8,128)(2,1)S(1)} %copy-done.6, bf16[16,104,128]{2,1,0:T(8,128)(2,1)S(1)} %collective-permute-done.2) | non-fusion elementwise | flops 212992 | bytes 1277952 | tf_op jit(solution)/shard_map/add | solution.py:206
  18.5 3.7 %all-to-all-start.2 = ((bf16[16,104,128]{2,1,0:T(8,128)(2,1)}), bf16[16,104,128]{2,1,0:T(8,128)(2,1)S(1)}, u32[]{:S(2)}, u32[]{:S(2)}) async-start(bf16[16,104,128]{2,1,0:T(8,128)(2,1)} %add.11), calls=%async_computation.2 | async-start | bytes 851968 | tf_op jit(solution)/shard_map/all_to_all | solution.py:180
  22.3 0.0 collective-permute-done
  22.3 0.9 %add.10 = bf16[16,104,128]{2,1,0:T(8,128)(2,1)} add(bf16[16,104,128]{2,1,0:T(8,128)(2,1)S(1)} %copy-done.5, bf16[16,104,128]{2,1,0:T(8,128)(2,1)S(1)} %collective-permute-done) | non-fusion elementwise | flops 212992 | bytes 1277952 | tf_op jit(solution)/shard_map/add | solution.py:207
  23.1 8.8 %all-to-all-done.2.got_ref = bf16[16,104,128]{2,1,0:T(8,128)(2,1)S(1)} async-done(((bf16[16,104,128]{2,1,0:T(8,128)(2,1)}), bf16[16,104,128]{2,1,0:T(8,128)(2,1)S(1)}, u32[]{:S(2)}, u32[]{:S(2)}) %all-to-all-start.2) | async-done | bytes 426016 | tf_op jit(solution)/shard_map/all_to_all | solution.py:180
  32.0 3.6 %all-to-all-start = ((bf16[16,104,128]{2,1,0:T(8,128)(2,1)}), bf16[16,104,128]{2,1,0:T(8,128)(2,1)S(1)}, u32[]{:S(2)}, u32[]{:S(2)}) async-start(bf16[16,104,128]{2,1,0:T(8,128)(2,1)} %add.10), calls=%async_computation | async-start | bytes 851968 | tf_op jit(solution)/shard_map/all_to_all | solution.py:180
  35.5 0.7 select_maximum_fusion.refs_1_
  36.2 0.7 select_maximum_fusion.1.refs_0_
  36.9 2.0 %shard_map.215 = (bf16[16,104,128]{2,1,0:T(8,128)(2,1)}, f32[40,320]{1,0:T(8,128)}, f32[40,320]{1,0:T(8,128)}, f32[8,128]{1,0:T(8,128)}, f32[8,128]{1,0:T(8,128)}) custom-call(bf16[16,104,128]{2,1,0:T(8,128)(2,1)} %copy-done.2, f32[40,320]{1,0:T(8,128)} %bitcast.33, f32[40,320]{1,0:T(8,128)} %bitcast.34, f32[8,128]{1,0:T(8,128)} %select_maximum_fusion.1.refs_0_, ...), custom_call_target="tpu_custom_call" | custom-call | tf_op jit(solution)/shard_map/pallas_call | solution.py:134
  38.9 5.4 %all-to-all-done.got_ref = bf16[16,104,128]{2,1,0:T(8,128)(2,1)S(1)} async-done(((bf16[16,104,128]{2,1,0:T(8,128)(2,1)}), bf16[16,104,128]{2,1,0:T(8,128)(2,1)S(1)}, u32[]{:S(2)}, u32[]{:S(2)}) %all-to-all-start) | async-done | bytes 426016 | tf_op jit(solution)/shard_map/all_to_all | solution.py:180
  44.4 3.6 %all-to-all-start.3 = ((bf16[16,104,128]{2,1,0:T(8,128)(2,1)}), bf16[16,104,128]{2,1,0:T(8,128)(2,1)S(1)}, u32[]{:S(2)}, u32[]{:S(2)}) async-start(bf16[16,104,128]{2,1,0:T(8,128)(2,1)} %get-tuple-element.29), calls=%async_computation.3 | async-start | bytes 851968 | tf_op jit(solution)/shard_map/all_to_all | solution.py:180
  48.0 2.0 %shard_map.212 = (bf16[16,104,128]{2,1,0:T(8,128)(2,1)}, f32[40,320]{1,0:T(8,128)}, f32[40,320]{1,0:T(8,128)}) custom-call(bf16[16,104,128]{2,1,0:T(8,128)(2,1)} %copy-done.3, f32[40,320]{1,0:T(8,128)} %param_ref.1, f32[40,320]{1,0:T(8,128)} %state_ref.1), custom_call_target="tpu_custom_call" | custom-call | tf_op jit(solution)/shard_map/pallas_call | solution.py:134
  50.0 6.4 %all-to-all-done.3.mine_ref = bf16[16,104,128]{2,1,0:T(8,128)(2,1)S(1)} async-done(((bf16[16,104,128]{2,1,0:T(8,128)(2,1)}), bf16[16,104,128]{2,1,0:T(8,128)(2,1)S(1)}, u32[]{:S(2)}, u32[]{:S(2)}) %all-to-all-start.3) | async-done | bytes 426016 | tf_op jit(solution)/shard_map/all_to_all | solution.py:180
  56.3 3.6 %all-to-all-start.1 = ((bf16[16,104,128]{2,1,0:T(8,128)(2,1)}), bf16[16,104,128]{2,1,0:T(8,128)(2,1)S(1)}, u32[]{:S(2)}, u32[]{:S(2)}) async-start(bf16[16,104,128]{2,1,0:T(8,128)(2,1)} %get-tuple-element.26), calls=%async_computation.1 | async-start | bytes 851968 | tf_op jit(solution)/shard_map/all_to_all | solution.py:180
  59.9 5.6 %collective-permute-start.3 = (bf16[16,104,128]{2,1,0:T(8,128)(2,1)S(1)}, bf16[16,104,128]{2,1,0:T(8,128)(2,1)S(1)}, u32[]{:S(2)}, u32[]{:S(2)}) collective-permute-start(bf16[16,104,128]{2,1,0:T(8,128)(2,1)S(1)} %all-to-all-done.3.mine_ref), channel_id=1, source_target_pairs={{0,16},{16,0},{1,17},{17,1},{2,18},{18,2},{3,19},{19,3},{4,20},{20... | collective-permute-start | bytes 1277960 | tf_op jit(solution)/shard_map/ppermute | solution.py:176
  65.5 2.8 %all-to-all-done.1.mine_ref = bf16[16,104,128]{2,1,0:T(8,128)(2,1)S(1)} async-done(((bf16[16,104,128]{2,1,0:T(8,128)(2,1)}), bf16[16,104,128]{2,1,0:T(8,128)(2,1)S(1)}, u32[]{:S(2)}, u32[]{:S(2)}) %all-to-all-start.1) | async-done | bytes 426016 | tf_op jit(solution)/shard_map/all_to_all | solution.py:180
  68.3 6.7 %collective-permute-start.1 = (bf16[16,104,128]{2,1,0:T(8,128)(2,1)S(1)}, bf16[16,104,128]{2,1,0:T(8,128)(2,1)S(1)}, u32[]{:S(2)}, u32[]{:S(2)}) collective-permute-start(bf16[16,104,128]{2,1,0:T(8,128)(2,1)S(1)} %all-to-all-done.1.mine_ref), channel_id=1, source_target_pairs={{0,16},{16,0},{1,17},{17,1},{2,18},{18,2},{3,19},{19,3},{4,20},{20... | collective-permute-start | bytes 1277960 | tf_op jit(solution)/shard_map/ppermute | solution.py:176
  75.0 1.4 %slice_bitcast_fusion = (f32[40]{0:T(128)}, f32[40]{0:T(128)}, f32[40]{0:T(128)}, f32[40]{0:T(128)}) fusion(f32[8,128]{1,0:T(8,128)} %get-tuple-element.35, f32[8,128]{1,0:T(8,128)} %get-tuple-element.32), kind=kLoop, calls=%fused_computation.13 | loop fusion | bytes 1280 | tf_op jit(solution)/shard_map/squeeze | solution.py:233
  76.3 0.0 collective-permute-done.3.other_ref
  76.4 0.1 fusion
  76.5 0.7 reshape_squeeze.6
  77.2 0.7 reshape_squeeze.7
  77.9 2.5 %shard_map.216 = bf16[320,1280]{1,0:T(8,128)(2,1)} custom-call(s32[1]{0:T(128)} %bitcast.core_ref, bf16[16,104,128]{2,1,0:T(8,128)(2,1)} %copy-done, bf16[16,104,128]{2,1,0:T(8,128)(2,1)} %copy-done.4), custom_call_target="tpu_custom_call" | custom-call | tf_op jit(solution)/shard_map/pallas_call | solution.py:166
  80.4 0.0 collective-permute-done.1.other_ref
  80.4 0.8 copy-done.7
  81.2 2.4 %shard_map.213 = bf16[320,1280]{1,0:T(8,128)(2,1)} custom-call(s32[1]{0:T(128)} %bitcast.core_ref, bf16[16,104,128]{2,1,0:T(8,128)(2,1)} %copy-done.1, bf16[16,104,128]{2,1,0:T(8,128)(2,1)} %copy-done.7), custom_call_target="tpu_custom_call" | custom-call | tf_op jit(solution)/shard_map/pallas_call | solution.py:166
  (25 shorter events, 0.1 us)
Async XLA Ops:
  3.8 13.8 %copy-start.6 = (bf16[16,104,128]{2,1,0:T(8,128)(2,1)S(1)}, bf16[16,104,128]{2,1,0:T(8,128)(2,1)}, u32[]{:S(2)}) copy-start(bf16[16,104,128]{2,1,0:T(8,128)(2,1)} %get-tuple-element.27) | copy-start | bytes 1277956
  3.8 13.8 %collective-permute-start.2 = (bf16[16,104,128]{2,1,0:T(8,128)(2,1)}, bf16[16,104,128]{2,1,0:T(8,128)(2,1)S(1)}, u32[]{:S(2)}, u32[]{:S(2)}) collective-permute-start(bf16[16,104,128]{2,1,0:T(8,128)(2,1)} %get-tuple-element.28), channel_id=1, source_target_pairs={{0,16},{16,0},{1,17},{17,1},{2,18},{18,2},{3,19},{19,3},{4,20},{20... | collective-permute-start | bytes 1277960 | tf_op jit(solution)/shard_map/ppermute | solution.py:176
  15.6 6.7 %copy-start.5 = (bf16[16,104,128]{2,1,0:T(8,128)(2,1)S(1)}, bf16[16,104,128]{2,1,0:T(8,128)(2,1)}, u32[]{:S(2)}) copy-start(bf16[16,104,128]{2,1,0:T(8,128)(2,1)} %get-tuple-element.24) | copy-start | bytes 1277956
  15.6 6.7 %collective-permute-start = (bf16[16,104,128]{2,1,0:T(8,128)(2,1)}, bf16[16,104,128]{2,1,0:T(8,128)(2,1)S(1)}, u32[]{:S(2)}, u32[]{:S(2)}) collective-permute-start(bf16[16,104,128]{2,1,0:T(8,128)(2,1)} %get-tuple-element.25), channel_id=1, source_target_pairs={{0,16},{16,0},{1,17},{17,1},{2,18},{18,2},{3,19},{19,3},{4,20},{20... | collective-permute-start | bytes 1277960 | tf_op jit(solution)/shard_map/ppermute | solution.py:176
  18.5 17.0 %copy-start.8 = (f32[40]{0:T(128)S(1)}, f32[40]{0:T(128)}, u32[]{:S(2)}) copy-start(f32[40]{0:T(128)} %param.23) | copy-start | bytes 484
  18.5 17.0 %copy-start.9 = (f32[40]{0:T(128)S(1)}, f32[40]{0:T(128)}, u32[]{:S(2)}) copy-start(f32[40]{0:T(128)} %param.22) | copy-start | bytes 484
  18.5 17.7 %copy-start.10 = (f32[40]{0:T(128)S(1)}, f32[40]{0:T(128)}, u32[]{:S(2)}) copy-start(f32[40]{0:T(128)} %param.19) | copy-start | bytes 484
  18.5 17.7 %copy-start.11 = (f32[40]{0:T(128)S(1)}, f32[40]{0:T(128)}, u32[]{:S(2)}) copy-start(f32[40]{0:T(128)} %param.18) | copy-start | bytes 484
  18.5 13.4 %all-to-all-start.2 = ((bf16[16,104,128]{2,1,0:T(8,128)(2,1)}), bf16[16,104,128]{2,1,0:T(8,128)(2,1)S(1)}, u32[]{:S(2)}, u32[]{:S(2)}) async-start(bf16[16,104,128]{2,1,0:T(8,128)(2,1)} %add.11), calls=%async_computation.2 | async-start | bytes 851968 | tf_op jit(solution)/shard_map/all_to_all | solution.py:180
  32.0 4.9 %copy-start.2 = (bf16[16,104,128]{2,1,0:T(8,128)(2,1)}, bf16[16,104,128]{2,1,0:T(8,128)(2,1)S(1)}, u32[]{:S(2)}) copy-start(bf16[16,104,128]{2,1,0:T(8,128)(2,1)S(1)} %all-to-all-done.2.got_ref) | copy-start | bytes 1277956
  32.0 12.4 %all-to-all-start = ((bf16[16,104,128]{2,1,0:T(8,128)(2,1)}), bf16[16,104,128]{2,1,0:T(8,128)(2,1)S(1)}, u32[]{:S(2)}, u32[]{:S(2)}) async-start(bf16[16,104,128]{2,1,0:T(8,128)(2,1)} %add.10), calls=%async_computation | async-start | bytes 851968 | tf_op jit(solution)/shard_map/all_to_all | solution.py:180
  44.4 3.6 %copy-start.3 = (bf16[16,104,128]{2,1,0:T(8,128)(2,1)}, bf16[16,104,128]{2,1,0:T(8,128)(2,1)S(1)}, u32[]{:S(2)}) copy-start(bf16[16,104,128]{2,1,0:T(8,128)(2,1)S(1)} %all-to-all-done.got_ref) | copy-start | bytes 1277956
  44.4 11.9 %all-to-all-start.3 = ((bf16[16,104,128]{2,1,0:T(8,128)(2,1)}), bf16[16,104,128]{2,1,0:T(8,128)(2,1)S(1)}, u32[]{:S(2)}, u32[]{:S(2)}) async-start(bf16[16,104,128]{2,1,0:T(8,128)(2,1)} %get-tuple-element.29), calls=%async_computation.3 | async-start | bytes 851968 | tf_op jit(solution)/shard_map/all_to_all | solution.py:180
  56.3 21.6 %copy-start = (bf16[16,104,128]{2,1,0:T(8,128)(2,1)}, bf16[16,104,128]{2,1,0:T(8,128)(2,1)S(1)}, u32[]{:S(2)}) copy-start(bf16[16,104,128]{2,1,0:T(8,128)(2,1)S(1)} %all-to-all-done.3.mine_ref) | copy-start | bytes 1277956
  56.3 12.0 %all-to-all-start.1 = ((bf16[16,104,128]{2,1,0:T(8,128)(2,1)}), bf16[16,104,128]{2,1,0:T(8,128)(2,1)S(1)}, u32[]{:S(2)}, u32[]{:S(2)}) async-start(bf16[16,104,128]{2,1,0:T(8,128)(2,1)} %get-tuple-element.26), calls=%async_computation.1 | async-start | bytes 851968 | tf_op jit(solution)/shard_map/all_to_all | solution.py:180
  59.9 16.5 %collective-permute-start.3 = (bf16[16,104,128]{2,1,0:T(8,128)(2,1)S(1)}, bf16[16,104,128]{2,1,0:T(8,128)(2,1)S(1)}, u32[]{:S(2)}, u32[]{:S(2)}) collective-permute-start(bf16[16,104,128]{2,1,0:T(8,128)(2,1)S(1)} %all-to-all-done.3.mine_ref), channel_id=1, source_target_pairs={{0,16},{16,0},{1,17},{17,1},{2,18},{18,2},{3,19},{19,3},{4,20},{20... | collective-permute-start | bytes 1277960 | tf_op jit(solution)/shard_map/ppermute | solution.py:176
  68.3 12.1 %copy-start.1 = (bf16[16,104,128]{2,1,0:T(8,128)(2,1)}, bf16[16,104,128]{2,1,0:T(8,128)(2,1)S(1)}, u32[]{:S(2)}) copy-start(bf16[16,104,128]{2,1,0:T(8,128)(2,1)S(1)} %all-to-all-done.1.mine_ref) | copy-start | bytes 1277956
  68.3 12.1 %collective-permute-start.1 = (bf16[16,104,128]{2,1,0:T(8,128)(2,1)S(1)}, bf16[16,104,128]{2,1,0:T(8,128)(2,1)S(1)}, u32[]{:S(2)}, u32[]{:S(2)}) collective-permute-start(bf16[16,104,128]{2,1,0:T(8,128)(2,1)S(1)} %all-to-all-done.1.mine_ref), channel_id=1, source_target_pairs={{0,16},{16,0},{1,17},{17,1},{2,18},{18,2},{3,19},{19,3},{4,20},{20... | collective-permute-start | bytes 1277960 | tf_op jit(solution)/shard_map/ppermute | solution.py:176
  76.4 1.6 %copy-start.4 = (bf16[16,104,128]{2,1,0:T(8,128)(2,1)}, bf16[16,104,128]{2,1,0:T(8,128)(2,1)S(1)}, u32[]{:S(2)}) copy-start(bf16[16,104,128]{2,1,0:T(8,128)(2,1)S(1)} %collective-permute-done.3.other_ref) | copy-start | bytes 1277956
  80.4 0.8 copy-start.7

commit v2 on v0

v2 whole, which is shorter than its diff:
```python
import functools

import jax
import jax.numpy as jnp
from jax import lax
from jax.experimental import pallas as pl
from jax.experimental.pallas import tpu as pltpu
from jax.sharding import Mesh
from jax.sharding import PartitionSpec as P

DP = ("dp_0", "dp_1", "dp_2")
CORE = "dp_2"

learn_rate = 0.1
hold_rate = 0.7

SHARE = 40
COLS = 320
WIDTH = 1280
FOLD = 24
ROWS = 2 * SHARE + FOLD
HALF = 64
TALL = COLS + 8
DEEP = 256
PIECES = 4

VMEM = pl.BlockSpec(memory_space=pltpu.VMEM)
SMEM = pl.BlockSpec(memory_space=pltpu.SMEM)
HBM = pl.BlockSpec(memory_space=pltpu.HBM)
ROOM = pltpu.CompilerParams(vmem_limit_bytes=8 * 2**20)
FIRST = pltpu.CompilerParams(vmem_limit_bytes=55500000)
SECOND = pltpu.CompilerParams(vmem_limit_bytes=55000000)


def eye(rows, cols, period=None):
    row = lax.broadcasted_iota(jnp.int32, (rows, cols), 0)
    col = lax.broadcasted_iota(jnp.int32, (rows, cols), 1)
    same = row == col
    if period:
        same = same | (row + period == col)
    return same.astype(jnp.float32).astype(jnp.bfloat16)


def times_transposed(a, b):
    return lax.dot_general(a, b, (((1,), (1,)), ((), ())), preferred_element_type=jnp.float32)


def low_lanes(rows):
    return lax.broadcasted_iota(jnp.int32, (rows, 128), 1) < HALF


def packed(first, second, tail, corner):
    upper = jnp.concatenate([tail[FOLD:], corner], axis=0)
    return jnp.concatenate([first, second, jnp.where(low_lanes(FOLD), tail[:FOLD], upper)], axis=0)


def pick_kernel(want_ref, up_ref, down_ref, norm_ref, bias_ref, out_ref, held, line, sems):
    step = COLS // PIECES

    def copies(matrix, vector):
        yield pltpu.make_async_copy(vector, line, sems.at[PIECES])
        for k in range(PIECES):
            rows = pl.ds(k * step, step)
            yield pltpu.make_async_copy(matrix.at[rows], held.at[rows], sems.at[k])

    up = want_ref[0] == 0

    @pl.when(up)
    def _():
        for copy in copies(up_ref, norm_ref):
            copy.start()

    @pl.when(jnp.logical_not(up))
    def _():
        for copy in copies(down_ref, bias_ref):
            copy.start()

    waits = list(copies(up_ref, norm_ref))
    waits[0].wait()
    out_ref[COLS:] = jnp.broadcast_to(line[...], (TALL - COLS, WIDTH)).astype(jnp.bfloat16)
    for k in range(PIECES):
        waits[k + 1].wait()
        rows = slice(k * step, (k + 1) * step)
        out_ref[rows] = held[rows].astype(jnp.bfloat16)


def pick(room, want, up, down, norm, bias):
    return pl.pallas_call(
        pick_kernel,
        in_specs=[SMEM, HBM, HBM, HBM, HBM],
        out_specs=VMEM,
        out_shape=jax.ShapeDtypeStruct((TALL, WIDTH), jnp.bfloat16),
        scratch_shapes=[
            pltpu.VMEM((COLS, WIDTH), jnp.float32),
            pltpu.VMEM((1, WIDTH), jnp.float32),
            pltpu.SemaphoreType.DMA((PIECES + 1,)),
        ],
        compiler_params=room,
        cost_estimate=pl.CostEstimate(flops=10**6, bytes_accessed=3 * 10**6, transcendentals=0),
    )(want, up, down, norm, bias)


def split_kernel(mine_ref, other_ref, out_ref, turned):
    one = eye(DEEP, DEEP)
    for k in range(WIDTH // DEEP):
        lanes = slice(k * DEEP, (k + 1) * DEEP)
        x = mine_ref[:COLS, lanes].astype(jnp.float32) + other_ref[:COLS, lanes].astype(jnp.float32)
        x = x.astype(jnp.bfloat16)
        x = jnp.concatenate([x, x[256:]], axis=0)
        turned[lanes] = times_transposed(one, x)
    line = mine_ref[COLS:].astype(jnp.float32) + other_ref[COLS:].astype(jnp.float32)
    zeros = jnp.zeros((8, HALF), jnp.float32)
    line = jnp.concatenate([zeros, line, zeros], axis=1)
    for d in range(WIDTH // SHARE):
        at = d * SHARE
        rows = slice(at, at + SHARE)
        out_ref[d] = packed(
            turned[rows, :128], turned[rows, 128:256], turned[rows, 256:], line[:, at : at + 128]
        ).astype(jnp.bfloat16)


def split(mine, other):
    return pl.pallas_call(
        split_kernel,
        in_specs=[VMEM, VMEM],
        out_specs=VMEM,
        out_shape=jax.ShapeDtypeStruct((WIDTH // SHARE, ROWS, 128), jnp.bfloat16),
        scratch_shapes=[pltpu.VMEM((WIDTH, 384), jnp.float32)],
        compiler_params=ROOM,
    )(mine, other)


def moved(total, state, param, rate):
    state_new = hold_rate * state + total * rate
    return state_new, param - learn_rate * state_new


def update_kernel(rate, got_ref, *refs):
    params, states, (half_ref, *nexts), news = refs[:4], refs[4:8], refs[8:13], refs[13:]
    halves, corner = [], jnp.zeros((8, 128), jnp.float32)
    row = lax.broadcasted_iota(jnp.int32, (8, 128), 0)
    gap = jnp.zeros((1, HALF), jnp.float32)
    for c in range(2):
        total = got_ref[c].astype(jnp.float32)
        for i in range(1, got_ref.shape[0] // 2):
            total += got_ref[2 * i + c].astype(jnp.float32)
        folded = total[2 * SHARE :]
        shifted = jnp.concatenate([folded[:, HALF:], folded[:, :HALF]], axis=1)
        tail = jnp.concatenate([folded[:FOLD, :HALF], shifted[: SHARE - FOLD, :HALF]], axis=0)
        mean = jnp.concatenate([total[:SHARE], total[SHARE : 2 * SHARE], tail], axis=1)
        new, nxt = moved(mean, states[c][...], params[c][...], rate)
        news[c][...] = new
        nexts[c][...] = nxt
        line = shifted[SHARE - FOLD : SHARE - FOLD + 1, :SHARE]
        new, line = moved(line, states[2 + c][...].reshape(1, SHARE), params[2 + c][...].reshape(1, SHARE), rate)
        news[2 + c][...] = new.reshape(SHARE)
        nexts[2 + c][...] = line.reshape(SHARE)
        line = jnp.concatenate([gap, line, gap[:, : HALF - SHARE]], axis=1)
        corner = jnp.where(row == c, jnp.broadcast_to(line, (8, 128)), corner)
        halves.append((nxt[:, :128], nxt[:, 128:256], jnp.concatenate([nxt[:, 256:], nxt[:, 256:]], axis=1)))
    halves = [packed(*half, corner).astype(jnp.bfloat16) for half in halves]
    for d in range(half_ref.shape[0]):
        half_ref[d] = halves[d % 2]


def update(rate, got, params, states):
    held = [jax.ShapeDtypeStruct(p.shape, jnp.float32) for p in params]
    return pl.pallas_call(
        functools.partial(update_kernel, rate),
        in_specs=[VMEM] * 9,
        out_specs=[VMEM] * 9,
        out_shape=[jax.ShapeDtypeStruct(got.shape, jnp.bfloat16), *held, *held],
        compiler_params=ROOM,
    )(got, *params, *states)


def put(ref, up_ref, down_ref, is_up, sem):
    @pl.when(is_up)
    def _():
        pltpu.make_async_copy(ref, up_ref, sem).start()

    @pl.when(jnp.logical_not(is_up))
    def _():
        pltpu.make_async_copy(ref, down_ref, sem).start()

    return pltpu.make_async_copy(ref, up_ref, sem)


def join_kernel(core_ref, blocks_ref, out_ref, lines_ref, up_ref, down_ref, wide, tails, sem):
    low = low_lanes(FOLD)
    upper = SHARE - FOLD
    pieces = []
    for d in range(WIDTH // SHARE):
        at = d * SHARE
        block = blocks_ref[d].astype(jnp.float32)
        wide[at : at + SHARE, :128] = block[:SHARE]
        wide[at : at + SHARE, 128:] = block[SHARE : 2 * SHARE]
        tail = block[2 * SHARE :]
        tails[at : at + FOLD] = jnp.where(low, tail, 0.0)
        tails[at + FOLD : at + SHARE] = jnp.where(low[:upper], 0.0, tail[:upper])
        pieces.append(tail[upper:, HALF : HALF + SHARE])
    one = eye(DEEP, DEEP)
    folded = eye(HALF, 128, HALF)
    for k in range(WIDTH // DEEP):
        lanes = slice(k * DEEP, (k + 1) * DEEP)
        out_ref[:256, lanes] = times_transposed(one, wide[lanes].astype(jnp.bfloat16)).astype(jnp.bfloat16)
        out_ref[256:, lanes] = times_transposed(folded, tails[lanes].astype(jnp.bfloat16)).astype(jnp.bfloat16)
    copy = put(out_ref, up_ref, down_ref, core_ref[0] == 0, sem)
    lines_ref[...] = jnp.concatenate(pieces, axis=1).astype(jnp.bfloat16)
    copy.wait()


def join(core, blocks):
    whole = jax.ShapeDtypeStruct((COLS, WIDTH), jnp.bfloat16)
    return pl.pallas_call(
        join_kernel,
        in_specs=[SMEM, VMEM],
        out_specs=[VMEM, VMEM, HBM, HBM],
        out_shape=[whole, jax.ShapeDtypeStruct((8, WIDTH), jnp.bfloat16), whole, whole],
        scratch_shapes=[
            pltpu.VMEM((WIDTH, 256), jnp.float32),
            pltpu.VMEM((WIDTH, 128), jnp.float32),
            pltpu.SemaphoreType.DMA,
        ],
        compiler_params=ROOM,
    )(core, blocks)


def place_kernel(core_ref, other_ref, up_in, down_in, up_ref, down_ref, sem):
    put(other_ref, up_ref, down_ref, core_ref[0] != 0, sem).wait()


def place(core, other, up, down):
    whole = jax.ShapeDtypeStruct((COLS, WIDTH), jnp.bfloat16)
    return pl.pallas_call(
        place_kernel,
        in_specs=[SMEM, VMEM, HBM, HBM],
        out_specs=[HBM, HBM],
        out_shape=[whole, whole],
        input_output_aliases={2: 0, 3: 1},
        scratch_shapes=[pltpu.SemaphoreType.DMA],
        compiler_params=ROOM,
    )(core, other, up, down)


def swapped(x):
    return lax.ppermute(x, CORE, [(0, 1), (1, 0)])


def exchanged(x):
    return lax.all_to_all(x, DP, 0, 0, tiled=True)


def body(
    slope_up,
    slope_down,
    slope_norm,
    slope_bias,
    param_up,
    param_down,
    param_norm,
    param_bias,
    state_up,
    state_down,
    state_norm,
    state_bias,
):
    rate = lax.axis_size(DP) ** (-0.5)
    core = lax.axis_index(CORE).astype(jnp.int32).reshape(1)
    slopes = (slope_up[0].T, slope_down[0], slope_norm, slope_bias)
    params = (param_up, param_down.T, param_norm, param_bias)
    states = (state_up, state_down.T, state_norm, state_bias)

    other = swapped(pick(FIRST, 1 - core, *slopes))
    mine = pick(SECOND, core, *slopes)
    half, *held = update(rate, exchanged(split(mine, other)), params, states)
    next_up, next_down, next_norm, next_bias, new_up, new_down, new_norm, new_bias = held
    mine, lines, up, down = join(core, exchanged(half))
    up, down = place(core, swapped(mine), up, down)
    return (
        up.T,
        down,
        lines[0],
        lines[1],
        next_up,
        next_down.T,
        next_norm,
        next_bias,
        new_up,
        new_down.T,
        new_norm,
        new_bias,
    )


def solution(mesh):
    torus = Mesh(mesh.devices.reshape(4, 4, 2, mesh.shape["tp"]), ("dp_0", "dp_1", "dp_2", "tp"))
    placed = (
        P(DP, None, "tp"),
        P(DP, "tp", None),
        P(DP, None),
        P(DP, None),
        P(DP, "tp"),
        P("tp", DP),
        P(DP),
        P(DP),
        P(DP, "tp"),
        P("tp", DP),
        P(DP),
        P(DP),
    )
    return jax.shard_map(
        body,
        mesh=torus,
        in_specs=placed,
        out_specs=(
            P(None, "tp"),
            P("tp", None),
            P(),
            P(),
            P(DP, "tp"),
            P("tp", DP),
            P(DP),
            P(DP),
            P(DP, "tp"),
            P("tp", DP),
            P(DP),
            P(DP),
        ),
        check_vma=False,
    )
```

time: 147 us -> 59.2 us (0.40)
  waiting for transfers between devices: 67.5 us -> 1.69 us
  starting transfers between devices: 42.6 us -> 11.2 us
  blocking collectives: 15.1 us -> 36.6 us
  local copies, waits for them, and re-layouts: 14.3 us -> 2.06 us
  Pallas kernels: 0 us -> 6.57 us
  other arithmetic: 5.57 us -> 0 us
    all_to_all x9 -> x0, waiting for transfers between devices: 67.5 us -> none  [the longest x4 41 us: sent_and_summed(): lax.all_to_all(split_up(shard, dim, length), axis, 0, 0, tiled=True)]
    all_to_all x9 -> x0, starting transfers between devices: 42.6 us -> none  [the longest x4 22.3 us: sent_and_summed(): lax.all_to_all(split_up(shard, dim, length), axis, 0, 0, tiled=True)]
    all_to_all x3 -> x2, blocking collectives: 15.1 us -> 36.6 us  [exchanged(): return lax.all_to_all(x, DP, 0, 0, tiled=True)]
    ppermute x0 -> x2, starting transfers between devices: none -> 11.2 us  [swapped(): return lax.ppermute(x, CORE, [(0, 1), (1, 0)])]
    unnamed x18 -> x24, local copies, waits for them, and re-layouts: 8.3 us -> 1.43 us
    pallas_call x0 -> x6, Pallas kernels: none -> 6.57 us  [the longest x2 2.92 us: pick(): pl.pallas_call(pick_kernel, in_specs=[SMEM, HBM, HBM, HBM, HBM], out_spec...]
    convert_element_type x6 -> x0, other arithmetic: 5.14 us -> none  [the longest x1 1.19 us: body(): next_norm.astype(jnp.bfloat16)]
    broadcast_in_dim x8 -> x0, local copies, waits for them, and re-layouts: 3.03 us -> none  [sent_to_all(): copies = jnp.broadcast_to(shard, (lax.axis_size(axis), *shard.shape))]
  transfers between devices with their start and end apart: 9 -> 2, of which waited for: 9 -> 2; matrix products, arithmetic and copies ran while one was open for 10% -> 1% of each run, Pallas kernels for 0% -> 2%
where the time goes in v2:
time: 59.2 us; the launch traced here: 58.9 us
  blocking collectives  36.6 us (62%)
  starting transfers between devices  11.2 us (19%)
  Pallas kernels  6.57 us (11%)
  local copies, waits for them, and re-layouts  2.06 us (3%)
  waiting for transfers between devices  1.69 us (3%)
  between operations  0.83 us (1%)
    all_to_all x2, blocking collectives, exchanged(): return lax.all_to_all(x, DP, 0, 0, tiled=True)  36.6 us
    ppermute x2, starting transfers between devices, swapped(): return lax.ppermute(x, CORE, [(0, 1), (1, 0)])  11.2 us
    pallas_call x2, Pallas kernels, pick(): pl.pallas_call(pick_kernel, in_specs=[SMEM, HBM, HBM, HBM, HBM], out_spec...  2.92 us
    ppermute x2, waiting for transfers between devices, swapped(): return lax.ppermute(x, CORE, [(0, 1), (1, 0)])  1.69 us
    unnamed x24, local copies, waits for them, and re-layouts  1.43 us
    pallas_call x1, Pallas kernels, join(): pl.pallas_call(join_kernel, in_specs=[SMEM, VMEM], out_specs=[VMEM, VMEM,...  1.38 us
  transfers between devices with their start and end apart: 2, of which 2 were waited for; matrix products, arithmetic and copies ran while one was open for 1% of the time, Pallas kernels for 2%

profile of v2, /device:TPU:1, one launch (start us, length us, event | category | flops | bytes accessed | tf_op | source)
XLA Modules:
  0.0 58.9 jit_solution(15610352275218109859)
XLA Ops:
  0.6 0.0 copy-start.4
  0.7 0.7 %copy-done.4 = f32[1,1280]{1,0:T(1,128)S(1)} copy-done((f32[1,1280]{1,0:T(1,128)S(1)}, f32[1,1280]{1,0:T(1,128)}, u32[]{:S(2)}) %copy-start.4) | copy-done | bytes 5144
  1.3 0.7 %copy-done.6 = f32[1,1280]{1,0:T(1,128)S(1)} copy-done((f32[1,1280]{1,0:T(1,128)S(1)}, f32[1,1280]{1,0:T(1,128)}, u32[]{:S(2)}) %copy-start.6) | copy-done | bytes 5144
  2.0 1.5 %shard_map.212 = bf16[328,1280]{1,0:T(8,128)(2,1)S(1)} custom-call(s32[1]{0:T(128)S(6)} %sub.3.want_ref, f32[320,1280]{1,0:T(8,128)} %bitcast.12, f32[320,1280]{1,0:T(8,128)} %bitcast.14, f32[1,1280]{1,0:T(1,128)S(1)} %copy-done.4, f32[1,1280]{1,0:T(1,128)S(1)} %copy-done.6), custom_call_target="tpu_custom_call" | custom-call | flops 1000000 | bytes 3000000 | tf_op jit(solution)/shard_map/pallas_call | solution.py:88
  3.5 8.7 %collective-permute-start = (bf16[328,1280]{1,0:T(8,128)(2,1)S(1)}, bf16[328,1280]{1,0:T(8,128)(2,1)S(1)}, u32[]{:S(2)}, u32[]{:S(2)}) collective-permute-start(bf16[328,1280]{1,0:T(8,128)(2,1)S(1)} %shard_map.212), channel_id=1, source_target_pairs={{0,16},{16,0},{1,17},{17,1},{2,18},{18,2},{3,19},{19,3},{4,20},{20... | collective-permute-start | bytes 2519048 | tf_op jit(solution)/shard_map/ppermute | solution.py:247
  12.3 0.0 copy-done.5
  12.3 0.0 copy-done.7
  12.3 1.5 %shard_map.211.mine_ref = bf16[328,1280]{1,0:T(8,128)(2,1)S(1)} custom-call(s32[1]{0:T(128)} %bitcast.want_ref.core_ref, f32[320,1280]{1,0:T(8,128)} %bitcast.13, f32[320,1280]{1,0:T(8,128)} %bitcast.15, f32[1,1280]{1,0:T(1,128)S(1)} %copy-done.5, f32[1,1280]{1,0:T(1,128)S(1)} %copy-done.7), custom_call_target="tpu_custom_call" | custom-call | flops 1000000 | bytes 3000000 | tf_op jit(solution)/shard_map/pallas_call | solution.py:88
  13.7 0.0 copy-start
  13.8 0.0 copy-start.1
  13.8 0.0 copy-start.2
  13.8 0.0 copy-start.3
  13.8 0.0 copy-start.8
  13.8 0.0 copy-start.9
  13.8 0.0 copy-start.10
  13.8 0.0 copy-start.11
  13.8 0.4 collective-permute-done.other_ref
  14.2 0.5 shard_map.213
  14.8 18.1 %all_to_all.10.got_ref = bf16[32,104,128]{2,1,0:T(8,128)(2,1)S(1)} all-to-all(bf16[32,104,128]{2,1,0:T(8,128)(2,1)S(1)} %shard_map.213), channel_id=1, replica_groups=mesh['dp_0'=4,'dp_1'=4,'dp_2'=2,'tp'=16] {'dp_0','dp_1','dp_2'}, dimensions={0} | all-to-all | bytes 1703936 | tf_op jit(solution)/shard_map/all_to_all | solution.py:251
  32.8 0.0 copy-done
  32.8 0.0 copy-done.1
  32.8 0.0 copy-done.2
  32.8 0.0 copy-done.3
  32.9 0.0 copy-done.8
  32.9 0.0 copy-done.9
  32.9 0.9 %shard_map.214 = (bf16[32,104,128]{2,1,0:T(8,128)(2,1)S(1)}, f32[40,320]{1,0:T(8,128)}, f32[40,320]{1,0:T(8,128)}, f32[40]{0:T(128)}, f32[40]{0:T(128)}, /*index...) custom-call(bf16[32,104,128]{2,1,0:T(8,128)(2,1)S(1)} %all_to_all.10.got_ref, f32[40,320]{1,0:T(8,128)S(1)} %copy-done, ...), custom_call_target="tpu_custom_call" | custom-call | tf_op jit(solution)/shard_map/pallas_call | solution.py:168
  33.8 18.5 %all_to_all.11.blocks_ref = bf16[32,104,128]{2,1,0:T(8,128)(2,1)S(1)} all-to-all(bf16[32,104,128]{2,1,0:T(8,128)(2,1)S(1)} %get-tuple-element.27), channel_id=1, replica_groups=mesh['dp_0'=4,'dp_1'=4,'dp_2'=2,'tp'=16] {'dp_0','dp_1','dp_2'}, dimensions={0} | all-to-all | bytes 1703936 | tf_op jit(solution)/shard_map/all_to_all | solution.py:251
  52.3 1.4 %shard_map.215 = (bf16[320,1280]{1,0:T(8,128)(2,1)S(1)}, bf16[8,1280]{1,0:T(8,128)(2,1)S(1)}, bf16[320,1280]{1,0:T(8,128)(2,1)}, bf16[320,1280]{1,0:T(8,128)(2,1)}) custom-call(s32[1]{0:T(128)} %bitcast.want_ref.core_ref, bf16[32,104,128]{2,1,0:T(8,128)(2,1)S(1)} %all_to_all.11.blocks_ref), custom_call_target="tpu_custom_call" | custom-call | tf_op jit(solution)/shard_map/pallas_call | solution.py:215
  53.6 2.4 %collective-permute-start.1 = (bf16[320,1280]{1,0:T(8,128)(2,1)S(1)}, bf16[320,1280]{1,0:T(8,128)(2,1)S(1)}, u32[]{:S(2)}, u32[]{:S(2)}) collective-permute-start(bf16[320,1280]{1,0:T(8,128)(2,1)S(1)} %get-tuple-element.28), channel_id=1, source_target_pairs={{0,16},{16,0},{1,17},{17,1},{2,18},{18,2},{3,19},{19,3},{4,20},{20... | collective-permute-start | bytes 2457608 | tf_op jit(solution)/shard_map/ppermute | solution.py:247
  56.1 0.6 %slice_reduce_fusion = (bf16[1280]{0:T(1024)(128)(2,1)}, bf16[1280]{0:T(1024)(128)(2,1)}) fusion(bf16[8,1280]{1,0:T(8,128)(2,1)S(1)} %get-tuple-element.33), kind=kLoop, calls=%fused_computation | loop fusion | bytes 10240 | tf_op jit(solution)/shard_map/slice | solution.py:284
  56.7 1.3 %collective-permute-done.1.other_ref = bf16[320,1280]{1,0:T(8,128)(2,1)S(1)} collective-permute-done((bf16[320,1280]{1,0:T(8,128)(2,1)S(1)}, bf16[320,1280]{1,0:T(8,128)(2,1)S(1)}, u32[]{:S(2)}, u32[]{:S(2)}) %collective-permute-start.1) | collective-permute-done | bytes 819232 | tf_op jit(solution)/shard_map/ppermute | solution.py:247
  58.0 0.9 %shard_map.216 = (bf16[320,1280]{1,0:T(8,128)(2,1)}, bf16[320,1280]{1,0:T(8,128)(2,1)}) custom-call(s32[1]{0:T(128)} %bitcast.want_ref.core_ref, bf16[320,1280]{1,0:T(8,128)(2,1)S(1)} %collective-permute-done.1.other_ref, bf16[320,1280]{1,0:T(8,128)(2,1)} %get-tuple-element.29.up_in, ...), custom_call_target="tpu_custom_call", output_to_operand_aliasing={{0}: (2, {}), {1}: (3, {})} | custom-call | tf_op jit(solution)/shard_map/pallas_call | solution.py:235
  (5 shorter events, 0.0 us)
Async XLA Ops:
  0.6 0.7 %copy-start.4 = (f32[1,1280]{1,0:T(1,128)S(1)}, f32[1,1280]{1,0:T(1,128)}, u32[]{:S(2)}) copy-start(f32[1,1280]{1,0:T(1,128)} %norm_ref.3) | copy-start | bytes 15364
  1.3 0.7 %copy-start.6 = (f32[1,1280]{1,0:T(1,128)S(1)}, f32[1,1280]{1,0:T(1,128)}, u32[]{:S(2)}) copy-start(f32[1,1280]{1,0:T(1,128)} %bias_ref.3) | copy-start | bytes 15364
  2.0 10.2 %copy-start.5 = (f32[1,1280]{1,0:T(1,128)S(1)}, f32[1,1280]{1,0:T(1,128)}, u32[]{:S(2)}) copy-start(f32[1,1280]{1,0:T(1,128)} %norm_ref.3) | copy-start | bytes 15364
  2.0 10.2 %copy-start.7 = (f32[1,1280]{1,0:T(1,128)S(1)}, f32[1,1280]{1,0:T(1,128)}, u32[]{:S(2)}) copy-start(f32[1,1280]{1,0:T(1,128)} %bias_ref.3) | copy-start | bytes 15364
  3.5 10.7 %collective-permute-start = (bf16[328,1280]{1,0:T(8,128)(2,1)S(1)}, bf16[328,1280]{1,0:T(8,128)(2,1)S(1)}, u32[]{:S(2)}, u32[]{:S(2)}) collective-permute-start(bf16[328,1280]{1,0:T(8,128)(2,1)S(1)} %shard_map.212), channel_id=1, source_target_pairs={{0,16},{16,0},{1,17},{17,1},{2,18},{18,2},{3,19},{19,3},{4,20},{20... | collective-permute-start | bytes 2519048 | tf_op jit(solution)/shard_map/ppermute | solution.py:247
  13.7 19.1 %copy-start = (f32[40,320]{1,0:T(8,128)S(1)}, f32[40,320]{1,0:T(8,128)}, u32[]{:S(2)}) copy-start(f32[40,320]{1,0:T(8,128)} %refs_0_.1) | copy-start | bytes 153604
  13.8 19.1 %copy-start.1 = (f32[320,40]{0,1:T(8,128)S(1)}, f32[320,40]{0,1:T(8,128)}, u32[]{:S(2)}) copy-start(f32[320,40]{0,1:T(8,128)} %param.17) | copy-start | bytes 153604
  13.8 19.1 %copy-start.2 = (f32[40,320]{1,0:T(8,128)S(1)}, f32[40,320]{1,0:T(8,128)}, u32[]{:S(2)}) copy-start(f32[40,320]{1,0:T(8,128)} %refs_4_.1) | copy-start | bytes 153604
  13.8 19.1 %copy-start.3 = (f32[320,40]{0,1:T(8,128)S(1)}, f32[320,40]{0,1:T(8,128)}, u32[]{:S(2)}) copy-start(f32[320,40]{0,1:T(8,128)} %param.21) | copy-start | bytes 153604
  13.8 19.1 %copy-start.8 = (f32[40]{0:T(128)S(1)}, f32[40]{0:T(128)}, u32[]{:S(2)}) copy-start(f32[40]{0:T(128)} %refs_2_.1) | copy-start | bytes 484
  13.8 19.1 %copy-start.9 = (f32[40]{0:T(128)S(1)}, f32[40]{0:T(128)}, u32[]{:S(2)}) copy-start(f32[40]{0:T(128)} %refs_3_.1) | copy-start | bytes 484
  13.8 19.1 %copy-start.10 = (f32[40]{0:T(128)S(1)}, f32[40]{0:T(128)}, u32[]{:S(2)}) copy-start(f32[40]{0:T(128)} %refs_6_.1) | copy-start | bytes 484
  13.8 19.1 %copy-start.11 = (f32[40]{0:T(128)S(1)}, f32[40]{0:T(128)}, u32[]{:S(2)}) copy-start(f32[40]{0:T(128)} %refs_7_.1) | copy-start | bytes 484
  53.6 4.4 %collective-permute-start.1 = (bf16[320,1280]{1,0:T(8,128)(2,1)S(1)}, bf16[320,1280]{1,0:T(8,128)(2,1)S(1)}, u32[]{:S(2)}, u32[]{:S(2)}) collective-permute-start(bf16[320,1280]{1,0:T(8,128)(2,1)S(1)} %get-tuple-element.28), channel_id=1, source_target_pairs={{0,16},{16,0},{1,17},{17,1},{2,18},{18,2},{3,19},{19,3},{4,20},{20... | collective-permute-start | bytes 2457608 | tf_op jit(solution)/shard_map/ppermute | solution.py:247

commit v3 on v2

--- a/solution.py
+++ b/solution.py
@@ -20,7 +20,6 @@
 FOLD = 24
 ROWS = 2 * SHARE + FOLD
 HALF = 64
-TALL = COLS + 8
 DEEP = 256
 PIECES = 4
 
@@ -54,11 +53,10 @@
     return jnp.concatenate([first, second, jnp.where(low_lanes(FOLD), tail[:FOLD], upper)], axis=0)
 
 
-def pick_kernel(want_ref, up_ref, down_ref, norm_ref, bias_ref, out_ref, held, line, sems):
+def pick_kernel(want_ref, up_ref, down_ref, out_ref, held, sems):
     step = COLS // PIECES
 
-    def copies(matrix, vector):
-        yield pltpu.make_async_copy(vector, line, sems.at[PIECES])
+    def copies(matrix):
         for k in range(PIECES):
             rows = pl.ds(k * step, step)
             yield pltpu.make_async_copy(matrix.at[rows], held.at[rows], sems.at[k])
@@ -67,48 +65,44 @@
 
     @pl.when(up)
     def _():
-        for copy in copies(up_ref, norm_ref):
+        for copy in copies(up_ref):
             copy.start()
 
     @pl.when(jnp.logical_not(up))
     def _():
-        for copy in copies(down_ref, bias_ref):
+        for copy in copies(down_ref):
             copy.start()
 
-    waits = list(copies(up_ref, norm_ref))
-    waits[0].wait()
-    out_ref[COLS:] = jnp.broadcast_to(line[...], (TALL - COLS, WIDTH)).astype(jnp.bfloat16)
-    for k in range(PIECES):
-        waits[k + 1].wait()
+    for k, copy in enumerate(copies(up_ref)):
+        copy.wait()
         rows = slice(k * step, (k + 1) * step)
         out_ref[rows] = held[rows].astype(jnp.bfloat16)
 
 
-def pick(room, want, up, down, norm, bias):
+def pick(room, want, up, down):
     return pl.pallas_call(
         pick_kernel,
-        in_specs=[SMEM, HBM, HBM, HBM, HBM],
+        in_specs=[SMEM, HBM, HBM],
         out_specs=VMEM,
-        out_shape=jax.ShapeDtypeStruct((TALL, WIDTH), jnp.bfloat16),
-        scratch_shapes=[
-            pltpu.VMEM((COLS, WIDTH), jnp.float32),
-            pltpu.VMEM((1, WIDTH), jnp.float32),
-            pltpu.SemaphoreType.DMA((PIECES + 1,)),
-        ],
+        out_shape=jax.ShapeDtypeStruct((COLS, WIDTH), jnp.bfloat16),
+        scratch_shapes=[pltpu.VMEM((COLS, WIDTH), jnp.float32), pltpu.SemaphoreType.DMA((PIECES,))],
         compiler_params=room,
         cost_estimate=pl.CostEstimate(flops=10**6, bytes_accessed=3 * 10**6, transcendentals=0),
-    )(want, up, down, norm, bias)
-
-
-def split_kernel(mine_ref, other_ref, out_ref, turned):
+    )(want, up, down)
+
+
+def split_kernel(mine_ref, other_ref, norm_ref, bias_ref, out_ref, turned):
     one = eye(DEEP, DEEP)
     for k in range(WIDTH // DEEP):
         lanes = slice(k * DEEP, (k + 1) * DEEP)
-        x = mine_ref[:COLS, lanes].astype(jnp.float32) + other_ref[:COLS, lanes].astype(jnp.float32)
+        x = mine_ref[:, lanes].astype(jnp.float32) + other_ref[:, lanes].astype(jnp.float32)
         x = x.astype(jnp.bfloat16)
         x = jnp.concatenate([x, x[256:]], axis=0)
         turned[lanes] = times_transposed(one, x)
-    line = mine_ref[COLS:].astype(jnp.float32) + other_ref[COLS:].astype(jnp.float32)
+    first_row = lax.broadcasted_iota(jnp.int32, (8, WIDTH), 0) == 0
+    line = jnp.where(
+        first_row, jnp.broadcast_to(norm_ref[...], (8, WIDTH)), jnp.broadcast_to(bias_ref[...], (8, WIDTH))
+    )
     zeros = jnp.zeros((8, HALF), jnp.float32)
     line = jnp.concatenate([zeros, line, zeros], axis=1)
     for d in range(WIDTH // SHARE):
@@ -119,15 +113,15 @@
         ).astype(jnp.bfloat16)
 
 
-def split(mine, other):
+def split(mine, other, norm, bias):
     return pl.pallas_call(
         split_kernel,
-        in_specs=[VMEM, VMEM],
+        in_specs=[VMEM] * 4,
         out_specs=VMEM,
         out_shape=jax.ShapeDtypeStruct((WIDTH // SHARE, ROWS, 128), jnp.bfloat16),
         scratch_shapes=[pltpu.VMEM((WIDTH, 384), jnp.float32)],
         compiler_params=ROOM,
-    )(mine, other)
+    )(mine, other, norm, bias)
 
 
 def moved(total, state, param, rate):
@@ -137,27 +131,30 @@
 
 def update_kernel(rate, got_ref, *refs):
     params, states, (half_ref, *nexts), news = refs[:4], refs[4:8], refs[8:13], refs[13:]
-    halves, corner = [], jnp.zeros((8, 128), jnp.float32)
-    row = lax.broadcasted_iota(jnp.int32, (8, 128), 0)
-    gap = jnp.zeros((1, HALF), jnp.float32)
+    halves, lines = [], 0.0
     for c in range(2):
         total = got_ref[c].astype(jnp.float32)
         for i in range(1, got_ref.shape[0] // 2):
             total += got_ref[2 * i + c].astype(jnp.float32)
         folded = total[2 * SHARE :]
         shifted = jnp.concatenate([folded[:, HALF:], folded[:, :HALF]], axis=1)
+        lines += shifted[SHARE - FOLD :]
         tail = jnp.concatenate([folded[:FOLD, :HALF], shifted[: SHARE - FOLD, :HALF]], axis=0)
         mean = jnp.concatenate([total[:SHARE], total[SHARE : 2 * SHARE], tail], axis=1)
         new, nxt = moved(mean, states[c][...], params[c][...], rate)
         news[c][...] = new
         nexts[c][...] = nxt
-        line = shifted[SHARE - FOLD : SHARE - FOLD + 1, :SHARE]
-        new, line = moved(line, states[2 + c][...].reshape(1, SHARE), params[2 + c][...].reshape(1, SHARE), rate)
+        halves.append((nxt[:, :128], nxt[:, 128:256], jnp.concatenate([nxt[:, 256:], nxt[:, 256:]], axis=1)))
+    row = lax.broadcasted_iota(jnp.int32, (8, 128), 0)
+    gap = jnp.zeros((1, HALF), jnp.float32)
+    corner = jnp.zeros((8, 128), jnp.float32)
+    for c in range(2):
+        state, param = (refs[2 + c][...].reshape(1, SHARE) for refs in (states, params))
+        new, line = moved(lines[c : c + 1, :SHARE], state, param, rate)
         news[2 + c][...] = new.reshape(SHARE)
         nexts[2 + c][...] = line.reshape(SHARE)
         line = jnp.concatenate([gap, line, gap[:, : HALF - SHARE]], axis=1)
         corner = jnp.where(row == c, jnp.broadcast_to(line, (8, 128)), corner)
-        halves.append((nxt[:, :128], nxt[:, 128:256], jnp.concatenate([nxt[:, 256:], nxt[:, 256:]], axis=1)))
     halves = [packed(*half, corner).astype(jnp.bfloat16) for half in halves]
     for d in range(half_ref.shape[0]):
         half_ref[d] = halves[d % 2]
@@ -174,19 +171,7 @@
     )(got, *params, *states)
 
 
-def put(ref, up_ref, down_ref, is_up, sem):
-    @pl.when(is_up)
-    def _():
-        pltpu.make_async_copy(ref, up_ref, sem).start()
-
-    @pl.when(jnp.logical_not(is_up))
-    def _():
-        pltpu.make_async_copy(ref, down_ref, sem).start()
-
-    return pltpu.make_async_copy(ref, up_ref, sem)
-
-
-def join_kernel(core_ref, blocks_ref, out_ref, lines_ref, up_ref, down_ref, wide, tails, sem):
+def join_kernel(blocks_ref, out_ref, lines_ref, wide, tails):
     low = low_lanes(FOLD)
     upper = SHARE - FOLD
     pieces = []
@@ -205,42 +190,59 @@
         lanes = slice(k * DEEP, (k + 1) * DEEP)
         out_ref[:256, lanes] = times_transposed(one, wide[lanes].astype(jnp.bfloat16)).astype(jnp.bfloat16)
         out_ref[256:, lanes] = times_transposed(folded, tails[lanes].astype(jnp.bfloat16)).astype(jnp.bfloat16)
-    copy = put(out_ref, up_ref, down_ref, core_ref[0] == 0, sem)
     lines_ref[...] = jnp.concatenate(pieces, axis=1).astype(jnp.bfloat16)
-    copy.wait()
-
-
-def join(core, blocks):
+
+
+def join(blocks):
+    return pl.pallas_call(
+        join_kernel,
+        in_specs=[VMEM],
+        out_specs=[VMEM, VMEM],
+        out_shape=[
+            jax.ShapeDtypeStruct((COLS, WIDTH), jnp.bfloat16),
+            jax.ShapeDtypeStruct((8, WIDTH), jnp.bfloat16),
+        ],
+        scratch_shapes=[pltpu.VMEM((WIDTH, 256), jnp.float32), pltpu.VMEM((WIDTH, 128), jnp.float32)],
+        compiler_params=ROOM,
+    )(blocks)
+
+
+def place_kernel(core_ref, ref, *refs):
+    up_ref, down_ref, sems = refs[-3:]
+    step = COLS // PIECES
+    is_up = core_ref[0] == 0
+
+    def copies(to):
+        for k in range(PIECES):
+            rows = pl.ds(k * step, step)
+            yield pltpu.make_async_copy(ref.at[rows], to.at[rows], sems.at[k])
+
+    @pl.when(is_up)
+    def _():
+        for copy in copies(up_ref):
+            copy.start()
+
+    @pl.when(jnp.logical_not(is_up))
+    def _():
+        for copy in copies(down_ref):
+            copy.start()
+
+    for copy in copies(up_ref):
+        copy.wait()
+
+
+def place(core, matrix, *held):
     whole = jax.ShapeDtypeStruct((COLS, WIDTH), jnp.bfloat16)
     return pl.pallas_call(
-        join_kernel,
-        in_specs=[SMEM, VMEM],
-        out_specs=[VMEM, VMEM, HBM, HBM],
-        out_shape=[whole, jax.ShapeDtypeStruct((8, WIDTH), jnp.bfloat16), whole, whole],
-        scratch_shapes=[
-            pltpu.VMEM((WIDTH, 256), jnp.float32),
-            pltpu.VMEM((WIDTH, 128), jnp.float32),
-            pltpu.SemaphoreType.DMA,
-        ],
-        compiler_params=ROOM,
-    )(core, blocks)
-
-
-def place_kernel(core_ref, other_ref, up_in, down_in, up_ref, down_ref, sem):
-    put(other_ref, up_ref, down_ref, core_ref[0] != 0, sem).wait()
-
-
-def place(core, other, up, down):
-    whole = jax.ShapeDtypeStruct((COLS, WIDTH), jnp.bfloat16)
-    return pl.pallas_call(
         place_kernel,
-        in_specs=[SMEM, VMEM, HBM, HBM],
+        in_specs=[SMEM, VMEM] + [HBM for _ in held],
         out_specs=[HBM, HBM],
         out_shape=[whole, whole],
-        input_output_aliases={2: 0, 3: 1},
-        scratch_shapes=[pltpu.SemaphoreType.DMA],
+        input_output_aliases={2: 0, 3: 1} if held else {},
+        scratch_shapes=[pltpu.SemaphoreType.DMA((PIECES,))],
         compiler_params=ROOM,
-    )(core, other, up, down)
+        cost_estimate=pl.CostEstimate(flops=0, bytes_accessed=2 * 10**6, transcendentals=0),
+    )(core, matrix, *held)
 
 
 def swapped(x):
@@ -267,16 +269,16 @@
 ):
     rate = lax.axis_size(DP) ** (-0.5)
     core = lax.axis_index(CORE).astype(jnp.int32).reshape(1)
-    slopes = (slope_up[0].T, slope_down[0], slope_norm, slope_bias)
+    slopes = (slope_up[0].T, slope_down[0])
     params = (param_up, param_down.T, param_norm, param_bias)
     states = (state_up, state_down.T, state_norm, state_bias)
 
     other = swapped(pick(FIRST, 1 - core, *slopes))
     mine = pick(SECOND, core, *slopes)
-    half, *held = update(rate, exchanged(split(mine, other)), params, states)
+    half, *held = update(rate, exchanged(split(mine, other, slope_norm, slope_bias)), params, states)
     next_up, next_down, next_norm, next_bias, new_up, new_down, new_norm, new_bias = held
-    mine, lines, up, down = join(core, exchanged(half))
-    up, down = place(core, swapped(mine), up, down)
+    mine, lines = join(exchanged(half))
+    up, down = place(1 - core, swapped(mine), *place(core, mine))
     return (
         up.T,
         down,

time: 59.2 us -> 56.9 us (0.961)
  local copies, waits for them, and re-layouts: 2.06 us -> 0.7 us
  waiting for transfers between devices: 1.69 us -> 0.76 us
    unnamed x24 -> x20, local copies, waits for them, and re-layouts: 1.43 us -> 0.06 us
    ppermute x2, waiting for transfers between devices: 1.69 us -> 0.76 us  [swapped(): return lax.ppermute(x, CORE, [(0, 1), (1, 0)])]
    pallas_call x5 -> x6, Pallas kernels: 5.71 us -> 5.71 us  [the longest x2 2.87 us: pick(): pl.pallas_call(pick_kernel, in_specs=[SMEM, HBM, HBM], out_specs=VMEM, ou...]
  transfers between devices with their start and end apart: 2 -> 2, of which waited for: 2 -> 2; matrix products, arithmetic and copies ran while one was open for 1% -> 1% of each run, Pallas kernels for 2% -> 4%
where the time goes in v3:
time: 56.9 us; the launch traced here: 56.6 us
  blocking collectives  36.6 us (64%)
  starting transfers between devices  11.2 us (20%)
  Pallas kernels  6.57 us (12%)
  between operations  0.82 us (1%)
  waiting for transfers between devices  0.76 us (1%)
  local copies, waits for them, and re-layouts  0.7 us (1%)
    all_to_all x2, blocking collectives, exchanged(): return lax.all_to_all(x, DP, 0, 0, tiled=True)  36.6 us
    ppermute x2, starting transfers between devices, swapped(): return lax.ppermute(x, CORE, [(0, 1), (1, 0)])  11.2 us
    pallas_call x2, Pallas kernels, pick(): pl.pallas_call(pick_kernel, in_specs=[SMEM, HBM, HBM], out_specs=VMEM, ou...  2.87 us
    pallas_call x2, Pallas kernels, place(): pl.pallas_call(place_kernel, in_specs=[SMEM, VMEM] + [HBM for _ in held],...  1.84 us
  transfers between devices with their start and end apart: 2, of which 2 were waited for; matrix products, arithmetic and copies ran while one was open for 1% of the time, Pallas kernels for 4%

profile of v3, /device:TPU:1, one launch (start us, length us, event | category | flops | bytes accessed | tf_op | source)
XLA Modules:
  0.0 56.6 jit_solution(12758411488364537763)
XLA Ops:
  0.6 1.4 %shard_map.212 = bf16[320,1280]{1,0:T(8,128)(2,1)S(1)} custom-call(s32[1]{0:T(128)S(6)} %sub.4.want_ref.core_ref, f32[320,1280]{1,0:T(8,128)} %bitcast.12, f32[320,1280]{1,0:T(8,128)} %bitcast.14), custom_call_target="tpu_custom_call" | custom-call | flops 1000000 | bytes 3000000 | tf_op jit(solution)/shard_map/pallas_call | solution.py:83
  2.1 0.0 copy-start.4
  2.1 0.0 copy-start.5
  2.1 8.8 %collective-permute-start = (bf16[320,1280]{1,0:T(8,128)(2,1)S(1)}, bf16[320,1280]{1,0:T(8,128)(2,1)S(1)}, u32[]{:S(2)}, u32[]{:S(2)}) collective-permute-start(bf16[320,1280]{1,0:T(8,128)(2,1)S(1)} %shard_map.212), channel_id=1, source_target_pairs={{0,16},{16,0},{1,17},{17,1},{2,18},{18,2},{3,19},{19,3},{4,20},{20... | collective-permute-start | bytes 2457608 | tf_op jit(solution)/shard_map/ppermute | solution.py:249
  10.9 1.4 %shard_map.211.mine_ref = bf16[320,1280]{1,0:T(8,128)(2,1)S(1)} custom-call(s32[1]{0:T(128)} %bitcast.want_ref.core_ref, f32[320,1280]{1,0:T(8,128)} %bitcast.13, f32[320,1280]{1,0:T(8,128)} %bitcast.15), custom_call_target="tpu_custom_call" | custom-call | flops 1000000 | bytes 3000000 | tf_op jit(solution)/shard_map/pallas_call | solution.py:83
  12.3 0.0 copy-start
  12.3 0.0 copy-start.1
  12.3 0.0 copy-start.2
  12.4 0.0 copy-start.3
  12.4 0.0 copy-start.6
  12.4 0.0 copy-start.7
  12.4 0.0 copy-start.8
  12.4 0.0 copy-start.9
  12.4 0.4 collective-permute-done.other_ref
  12.8 0.0 copy-done.4
  12.8 0.0 copy-done.5
  12.8 0.5 shard_map.213
  13.3 18.1 %all_to_all.10.got_ref = bf16[32,104,128]{2,1,0:T(8,128)(2,1)S(1)} all-to-all(bf16[32,104,128]{2,1,0:T(8,128)(2,1)S(1)} %shard_map.213), channel_id=1, replica_groups=mesh['dp_0'=4,'dp_1'=4,'dp_2'=2,'tp'=16] {'dp_0','dp_1','dp_2'}, dimensions={0} | all-to-all | bytes 1703936 | tf_op jit(solution)/shard_map/all_to_all | solution.py:253
  31.4 0.0 copy-done
  31.4 0.0 copy-done.3
  31.4 0.0 copy-done.6
  31.5 0.0 copy-done.7
  31.5 0.0 copy-done.8
  31.5 0.0 copy-done.9
  31.5 0.9 %shard_map.214 = (bf16[32,104,128]{2,1,0:T(8,128)(2,1)S(1)}, f32[40,320]{1,0:T(8,128)}, f32[40,320]{1,0:T(8,128)}, f32[40]{0:T(128)}, f32[40]{0:T(128)}, /*index...) custom-call(bf16[32,104,128]{2,1,0:T(8,128)(2,1)S(1)} %all_to_all.10.got_ref, f32[40,320]{1,0:T(8,128)S(1)} %copy-done, ...), custom_call_target="tpu_custom_call" | custom-call | tf_op jit(solution)/shard_map/pallas_call | solution.py:165
  32.3 18.5 %all_to_all.11.blocks_ref = bf16[32,104,128]{2,1,0:T(8,128)(2,1)S(1)} all-to-all(bf16[32,104,128]{2,1,0:T(8,128)(2,1)S(1)} %get-tuple-element.27), channel_id=1, replica_groups=mesh['dp_0'=4,'dp_1'=4,'dp_2'=2,'tp'=16] {'dp_0','dp_1','dp_2'}, dimensions={0} | all-to-all | bytes 1703936 | tf_op jit(solution)/shard_map/all_to_all | solution.py:253
  50.8 0.5 shard_map.215
  51.3 2.4 %collective-permute-start.1 = (bf16[320,1280]{1,0:T(8,128)(2,1)S(1)}, bf16[320,1280]{1,0:T(8,128)(2,1)S(1)}, u32[]{:S(2)}, u32[]{:S(2)}) collective-permute-start(bf16[320,1280]{1,0:T(8,128)(2,1)S(1)} %get-tuple-element.28.ref), channel_id=1, source_target_pairs={{0,16},{16,0},{1,17},{17,1},{2,18},{18,2},{3,19},{19,3},{4,20},{20... | collective-permute-start | bytes 2457608 | tf_op jit(solution)/shard_map/ppermute | solution.py:249
  53.7 0.9 %shard_map.216 = (bf16[320,1280]{1,0:T(8,128)(2,1)}, bf16[320,1280]{1,0:T(8,128)(2,1)}) custom-call(s32[1]{0:T(128)} %bitcast.want_ref.core_ref, bf16[320,1280]{1,0:T(8,128)(2,1)S(1)} %get-tuple-element.28.ref), custom_call_target="tpu_custom_call" | custom-call | bytes 2000000 | tf_op jit(solution)/shard_map/pallas_call | solution.py:236
  54.7 0.6 %slice_reduce_fusion = (bf16[1280]{0:T(1024)(128)(2,1)}, bf16[1280]{0:T(1024)(128)(2,1)}) fusion(bf16[8,1280]{1,0:T(8,128)(2,1)S(1)} %get-tuple-element.33), kind=kLoop, calls=%fused_computation | loop fusion | bytes 10240 | tf_op jit(solution)/shard_map/slice | solution.py:286
  55.3 0.4 collective-permute-done.1.ref
  55.7 0.9 %shard_map.217 = (bf16[320,1280]{1,0:T(8,128)(2,1)}, bf16[320,1280]{1,0:T(8,128)(2,1)}) custom-call(s32[1]{0:T(128)S(6)} %sub.4.want_ref.core_ref, bf16[320,1280]{1,0:T(8,128)(2,1)S(1)} %collective-permute-done.1.ref, bf16[320,1280]{1,0:T(8,128)(2,1)} %get-tuple-element.29.refs_0_, ...), custom_call_target="tpu_custom_call", output_to_operand_aliasing={{0}: (2, {}), {1}: (3, {})} | custom-call | bytes 2000000 | tf_op jit(solution)/shard_map/pallas_call | solution.py:236
  (2 shorter events, 0.0 us)
Async XLA Ops:
  2.1 10.7 %copy-start.4 = (f32[1,1280]{1,0:T(1,128)S(1)}, f32[1,1280]{1,0:T(1,128)}, u32[]{:S(2)}) copy-start(f32[1,1280]{1,0:T(1,128)} %norm_ref.1) | copy-start | bytes 15364
  2.1 10.7 %copy-start.5 = (f32[1,1280]{1,0:T(1,128)S(1)}, f32[1,1280]{1,0:T(1,128)}, u32[]{:S(2)}) copy-start(f32[1,1280]{1,0:T(1,128)} %bias_ref.1) | copy-start | bytes 15364
  2.1 10.7 %collective-permute-start = (bf16[320,1280]{1,0:T(8,128)(2,1)S(1)}, bf16[320,1280]{1,0:T(8,128)(2,1)S(1)}, u32[]{:S(2)}, u32[]{:S(2)}) collective-permute-start(bf16[320,1280]{1,0:T(8,128)(2,1)S(1)} %shard_map.212), channel_id=1, source_target_pairs={{0,16},{16,0},{1,17},{17,1},{2,18},{18,2},{3,19},{19,3},{4,20},{20... | collective-permute-start | bytes 2457608 | tf_op jit(solution)/shard_map/ppermute | solution.py:249
  12.3 19.1 %copy-start = (f32[40,320]{1,0:T(8,128)S(1)}, f32[40,320]{1,0:T(8,128)}, u32[]{:S(2)}) copy-start(f32[40,320]{1,0:T(8,128)} %refs_0_.1) | copy-start | bytes 153604
  12.3 19.1 %copy-start.1 = (f32[320,40]{0,1:T(8,128)S(1)}, f32[320,40]{0,1:T(8,128)}, u32[]{:S(2)}) copy-start(f32[320,40]{0,1:T(8,128)} %param.17) | copy-start | bytes 153604
  12.3 19.1 %copy-start.2 = (f32[40,320]{1,0:T(8,128)S(1)}, f32[40,320]{1,0:T(8,128)}, u32[]{:S(2)}) copy-start(f32[40,320]{1,0:T(8,128)} %refs_4_.1) | copy-start | bytes 153604
  12.4 19.1 %copy-start.3 = (f32[320,40]{0,1:T(8,128)S(1)}, f32[320,40]{0,1:T(8,128)}, u32[]{:S(2)}) copy-start(f32[320,40]{0,1:T(8,128)} %param.21) | copy-start | bytes 153604
  12.4 19.1 %copy-start.6 = (f32[40]{0:T(128)S(1)}, f32[40]{0:T(128)}, u32[]{:S(2)}) copy-start(f32[40]{0:T(128)} %refs_2_.1) | copy-start | bytes 484
  12.4 19.1 %copy-start.7 = (f32[40]{0:T(128)S(1)}, f32[40]{0:T(128)}, u32[]{:S(2)}) copy-start(f32[40]{0:T(128)} %refs_3_.1) | copy-start | bytes 484
  12.4 19.1 %copy-start.8 = (f32[40]{0:T(128)S(1)}, f32[40]{0:T(128)}, u32[]{:S(2)}) copy-start(f32[40]{0:T(128)} %refs_6_.1) | copy-start | bytes 484
  12.4 19.1 %copy-start.9 = (f32[40]{0:T(128)S(1)}, f32[40]{0:T(128)}, u32[]{:S(2)}) copy-start(f32[40]{0:T(128)} %refs_7_.1) | copy-start | bytes 484
  51.3 4.4 %collective-permute-start.1 = (bf16[320,1280]{1,0:T(8,128)(2,1)S(1)}, bf16[320,1280]{1,0:T(8,128)(2,1)S(1)}, u32[]{:S(2)}, u32[]{:S(2)}) collective-permute-start(bf16[320,1280]{1,0:T(8,128)(2,1)S(1)} %get-tuple-element.28.ref), channel_id=1, source_target_pairs={{0,16},{16,0},{1,17},{17,1},{2,18},{18,2},{3,19},{19,3},{4,20},{20... | collective-permute-start | bytes 2457608 | tf_op jit(solution)/shard_map/ppermute | solution.py:249

commit v4 on v3

--- a/solution.py
+++ b/solution.py
@@ -171,78 +171,80 @@
     )(got, *params, *states)
 
 
-def join_kernel(blocks_ref, out_ref, lines_ref, wide, tails):
+def join_kernel(small, core_ref, blocks_ref, *refs):
+    wide, tails, out, sems = refs[-4:]
+    if small:
+        held, (lines_ref, up_ref, down_ref), placed = refs[:small], refs[small : small + 3], refs[small + 3 : -4]
+    else:
+        up_ref, down_ref = refs[2:4]
+        held, placed = (), ()
+    writes = [pltpu.make_async_copy(h, p, sems.at[i]) for i, (h, p) in enumerate(zip(held, placed))]
+    for write in writes:
+        write.start()
+    is_up = core_ref[0] == 0
+
+    def copy(to, k):
+        lanes = pl.ds(k * DEEP, DEEP)
+        return pltpu.make_async_copy(out.at[:, lanes], to.at[:, lanes], sems.at[small + k])
+
     low = low_lanes(FOLD)
     upper = SHARE - FOLD
     pieces = []
-    for d in range(WIDTH // SHARE):
-        at = d * SHARE
-        block = blocks_ref[d].astype(jnp.float32)
-        wide[at : at + SHARE, :128] = block[:SHARE]
-        wide[at : at + SHARE, 128:] = block[SHARE : 2 * SHARE]
-        tail = block[2 * SHARE :]
-        tails[at : at + FOLD] = jnp.where(low, tail, 0.0)
-        tails[at + FOLD : at + SHARE] = jnp.where(low[:upper], 0.0, tail[:upper])
-        pieces.append(tail[upper:, HALF : HALF + SHARE])
     one = eye(DEEP, DEEP)
     folded = eye(HALF, 128, HALF)
+    d = 0
     for k in range(WIDTH // DEEP):
+        while d * SHARE < (k + 1) * DEEP:
+            at = d * SHARE
+            block = blocks_ref[d].astype(jnp.float32)
+            wide[at : at + SHARE, :128] = block[:SHARE]
+            wide[at : at + SHARE, 128:] = block[SHARE : 2 * SHARE]
+            tail = block[2 * SHARE :]
+            tails[at : at + FOLD] = jnp.where(low, tail, 0.0)
+            tails[at + FOLD : at + SHARE] = jnp.where(low[:upper], 0.0, tail[:upper])
+            if small:
+                pieces.append(tail[upper:, HALF : HALF + SHARE])
+            d += 1
         lanes = slice(k * DEEP, (k + 1) * DEEP)
-        out_ref[:256, lanes] = times_transposed(one, wide[lanes].astype(jnp.bfloat16)).astype(jnp.bfloat16)
-        out_ref[256:, lanes] = times_transposed(folded, tails[lanes].astype(jnp.bfloat16)).astype(jnp.bfloat16)
-    lines_ref[...] = jnp.concatenate(pieces, axis=1).astype(jnp.bfloat16)
-
-
-def join(blocks):
+        out[:256, lanes] = times_transposed(one, wide[lanes].astype(jnp.bfloat16)).astype(jnp.bfloat16)
+        out[256:, lanes] = times_transposed(folded, tails[lanes].astype(jnp.bfloat16)).astype(jnp.bfloat16)
+
+        @pl.when(is_up)
+        def _():
+            copy(up_ref, k).start()
+
+        @pl.when(jnp.logical_not(is_up))
+        def _():
+            copy(down_ref, k).start()
+
+    if small:
+        lines_ref[...] = jnp.concatenate(pieces, axis=1).astype(jnp.bfloat16)
+    for write in writes:
+        write.wait()
+    for k in range(WIDTH // DEEP):
+        copy(up_ref, k).wait()
+
+
+def join(core, blocks, small=(), begun=()):
+    whole = jax.ShapeDtypeStruct((COLS, WIDTH), jnp.bfloat16)
+    lines = jax.ShapeDtypeStruct((8, WIDTH), jnp.bfloat16)
     return pl.pallas_call(
-        join_kernel,
-        in_specs=[VMEM],
-        out_specs=[VMEM, VMEM],
-        out_shape=[
-            jax.ShapeDtypeStruct((COLS, WIDTH), jnp.bfloat16),
-            jax.ShapeDtypeStruct((8, WIDTH), jnp.bfloat16),
+        functools.partial(join_kernel, len(small)),
+        in_specs=[SMEM, VMEM] + [VMEM for _ in small] + [HBM for _ in begun],
+        out_specs=[VMEM for _ in small[:1]] + [HBM, HBM] + [HBM for _ in small],
+        out_shape=[lines for _ in small[:1]]
+        + [whole, whole]
+        + [jax.ShapeDtypeStruct(x.shape, x.dtype) for x in small],
+        input_output_aliases={2: 0, 3: 1} if begun else {},
+        scratch_shapes=[
+            pltpu.VMEM((WIDTH, 256), jnp.float32),
+            pltpu.VMEM((WIDTH, 128), jnp.float32),
+            pltpu.VMEM((COLS, WIDTH), jnp.bfloat16),
+            pltpu.SemaphoreType.DMA((len(small) + WIDTH // DEEP,)),
         ],
-        scratch_shapes=[pltpu.VMEM((WIDTH, 256), jnp.float32), pltpu.VMEM((WIDTH, 128), jnp.float32)],
         compiler_params=ROOM,
-    )(blocks)
-
-
-def place_kernel(core_ref, ref, *refs):
-    up_ref, down_ref, sems = refs[-3:]
-    step = COLS // PIECES
-    is_up = core_ref[0] == 0
-
-    def copies(to):
-        for k in range(PIECES):
-            rows = pl.ds(k * step, step)
-            yield pltpu.make_async_copy(ref.at[rows], to.at[rows], sems.at[k])
-
-    @pl.when(is_up)
-    def _():
-        for copy in copies(up_ref):
-            copy.start()
-
-    @pl.when(jnp.logical_not(is_up))
-    def _():
-        for copy in copies(down_ref):
-            copy.start()
-
-    for copy in copies(up_ref):
-        copy.wait()
-
-
-def place(core, matrix, *held):
-    whole = jax.ShapeDtypeStruct((COLS, WIDTH), jnp.bfloat16)
-    return pl.pallas_call(
-        place_kernel,
-        in_specs=[SMEM, VMEM] + [HBM for _ in held],
-        out_specs=[HBM, HBM],
-        out_shape=[whole, whole],
-        input_output_aliases={2: 0, 3: 1} if held else {},
-        scratch_shapes=[pltpu.SemaphoreType.DMA((PIECES,))],
-        compiler_params=ROOM,
-        cost_estimate=pl.CostEstimate(flops=0, bytes_accessed=2 * 10**6, transcendentals=0),
-    )(core, matrix, *held)
+        cost_estimate=pl.CostEstimate(flops=10**9, bytes_accessed=2 * 10**6, transcendentals=0),
+    )(core, blocks, *small, *begun)
 
 
 def swapped(x):
@@ -276,9 +278,12 @@
     other = swapped(pick(FIRST, 1 - core, *slopes))
     mine = pick(SECOND, core, *slopes)
     half, *held = update(rate, exchanged(split(mine, other, slope_norm, slope_bias)), params, states)
-    next_up, next_down, next_norm, next_bias, new_up, new_down, new_norm, new_bias = held
-    mine, lines = join(exchanged(half))
-    up, down = place(1 - core, swapped(mine), *place(core, mine))
+    mine = exchanged(half)
+    other = swapped(mine)
+    lines, *begun, next_up, next_down, next_norm, next_bias, new_up, new_down, new_norm, new_bias = join(
+        core, mine, held
+    )
+    up, down = join(1 - core, other, begun=begun)
     return (
         up.T,
         down,

time: 56.9 us -> 56.2 us (0.988)
    pallas_call x3 -> x2, Pallas kernels: 2.31 us -> 2.5 us  [join(): pl.pallas_call(functools.partial(join_kernel, len(small)), in_specs=[SMEM...]
  transfers between devices with their start and end apart: 2 -> 2, of which waited for: 2 -> 1; matrix products, arithmetic and copies ran while one was open for 1% -> 1% of each run, Pallas kernels for 4% -> 5%
where the time goes in v4:
time: 56.2 us; the launch traced here: 55.9 us
  blocking collectives  36.6 us (65%)
  starting transfers between devices  11.2 us (20%)
  Pallas kernels  6.19 us (11%)
  between operations  0.82 us (1%)
  local copies, waits for them, and re-layouts  0.7 us (1%)
    all_to_all x2, blocking collectives, exchanged(): return lax.all_to_all(x, DP, 0, 0, tiled=True)  36.6 us
    ppermute x2, starting transfers between devices, swapped(): return lax.ppermute(x, CORE, [(0, 1), (1, 0)])  11.2 us
    pallas_call x2, Pallas kernels, pick(): pl.pallas_call(pick_kernel, in_specs=[SMEM, HBM, HBM], out_specs=VMEM, ou...  2.87 us
    pallas_call x2, Pallas kernels, join(): pl.pallas_call(functools.partial(join_kernel, len(small)), in_specs=[SMEM...  2.5 us
  transfers between devices with their start and end apart: 2, of which 1 were waited for; matrix products, arithmetic and copies ran while one was open for 1% of the time, Pallas kernels for 5%

profile of v4, /device:TPU:1, one launch (start us, length us, event | category | flops | bytes accessed | tf_op | source)
XLA Modules:
  0.0 55.9 jit_solution(8519382529960715583)
XLA Ops:
  0.6 1.4 %shard_map.212 = bf16[320,1280]{1,0:T(8,128)(2,1)S(1)} custom-call(s32[1]{0:T(128)S(6)} %sub.4.want_ref.core_ref, f32[320,1280]{1,0:T(8,128)} %bitcast.12, f32[320,1280]{1,0:T(8,128)} %bitcast.14), custom_call_target="tpu_custom_call" | custom-call | flops 1000000 | bytes 3000000 | tf_op jit(solution)/shard_map/pallas_call | solution.py:83
  2.1 0.0 copy-start.4
  2.1 0.0 copy-start.5
  2.1 8.8 %collective-permute-start = (bf16[320,1280]{1,0:T(8,128)(2,1)S(1)}, bf16[320,1280]{1,0:T(8,128)(2,1)S(1)}, u32[]{:S(2)}, u32[]{:S(2)}) collective-permute-start(bf16[320,1280]{1,0:T(8,128)(2,1)S(1)} %shard_map.212), channel_id=1, source_target_pairs={{0,16},{16,0},{1,17},{17,1},{2,18},{18,2},{3,19},{19,3},{4,20},{20... | collective-permute-start | bytes 2457608 | tf_op jit(solution)/shard_map/ppermute | solution.py:251
  10.9 1.4 %shard_map.211.mine_ref = bf16[320,1280]{1,0:T(8,128)(2,1)S(1)} custom-call(s32[1]{0:T(128)} %bitcast.want_ref.core_ref, f32[320,1280]{1,0:T(8,128)} %bitcast.13, f32[320,1280]{1,0:T(8,128)} %bitcast.15), custom_call_target="tpu_custom_call" | custom-call | flops 1000000 | bytes 3000000 | tf_op jit(solution)/shard_map/pallas_call | solution.py:83
  12.3 0.0 copy-start
  12.3 0.0 copy-start.1
  12.3 0.0 copy-start.2
  12.4 0.0 copy-start.3
  12.4 0.0 copy-start.6
  12.4 0.0 copy-start.7
  12.4 0.0 copy-start.8
  12.4 0.0 copy-start.9
  12.4 0.4 collective-permute-done.other_ref
  12.8 0.0 copy-done.4
  12.8 0.0 copy-done.5
  12.8 0.5 shard_map.213
  13.3 18.1 %all_to_all.10.got_ref = bf16[32,104,128]{2,1,0:T(8,128)(2,1)S(1)} all-to-all(bf16[32,104,128]{2,1,0:T(8,128)(2,1)S(1)} %shard_map.213), channel_id=1, replica_groups=mesh['dp_0'=4,'dp_1'=4,'dp_2'=2,'tp'=16] {'dp_0','dp_1','dp_2'}, dimensions={0} | all-to-all | bytes 1703936 | tf_op jit(solution)/shard_map/all_to_all | solution.py:255
  31.4 0.0 copy-done
  31.4 0.0 copy-done.1
  31.4 0.0 copy-done.2
  31.4 0.0 copy-done.3
  31.4 0.0 copy-done.6
  31.5 0.0 copy-done.7
  31.5 0.0 copy-done.8
  31.5 0.3 shard_map.214
  31.8 18.5 %all_to_all.11.blocks_ref = bf16[32,104,128]{2,1,0:T(8,128)(2,1)S(1)} all-to-all(bf16[32,104,128]{2,1,0:T(8,128)(2,1)S(1)} %get-tuple-element.34), channel_id=1, replica_groups=mesh['dp_0'=4,'dp_1'=4,'dp_2'=2,'tp'=16] {'dp_0','dp_1','dp_2'}, dimensions={0} | all-to-all | bytes 1703936 | tf_op jit(solution)/shard_map/all_to_all | solution.py:255
  50.3 2.4 %collective-permute-start.1 = (bf16[32,104,128]{2,1,0:T(8,128)(2,1)S(1)}, bf16[32,104,128]{2,1,0:T(8,128)(2,1)S(1)}, u32[]{:S(2)}, u32[]{:S(2)}) collective-permute-start(bf16[32,104,128]{2,1,0:T(8,128)(2,1)S(1)} %all_to_all.11.blocks_ref), channel_id=1, source_target_pairs={{0,16},{16,0},{1,17},{17,1},{2,18},{18,2},{3,19},{19,3},{4,20},{20... | collective-permute-start | bytes 2555912 | tf_op jit(solution)/shard_map/ppermute | solution.py:251
  52.7 1.3 %shard_map.215 = (bf16[8,1280]{1,0:T(8,128)(2,1)S(1)}, bf16[320,1280]{1,0:T(8,128)(2,1)}, bf16[320,1280]{1,0:T(8,128)(2,1)}, f32[40,320]{1,0:T(8,128)}, f32[40,3...) custom-call(s32[1]{0:T(128)} %bitcast.want_ref.core_ref, ...), custom_call_target="tpu_custom_call" | custom-call | flops 1000000000 | bytes 2000000 | tf_op jit(solution)/shard_map/pallas_call | solution.py:231
  54.0 0.6 %slice_reduce_fusion = (bf16[1280]{0:T(1024)(128)(2,1)}, bf16[1280]{0:T(1024)(128)(2,1)}) fusion(bf16[8,1280]{1,0:T(8,128)(2,1)S(1)} %get-tuple-element.47), kind=kLoop, calls=%fused_computation | loop fusion | bytes 10240 | tf_op jit(solution)/shard_map/slice | solution.py:291
  54.6 0.1 collective-permute-done.1.blocks_ref
  54.7 1.2 %shard_map.216 = (bf16[320,1280]{1,0:T(8,128)(2,1)}, bf16[320,1280]{1,0:T(8,128)(2,1)}) custom-call(s32[1]{0:T(128)S(6)} %sub.4.want_ref.core_ref, bf16[32,104,128]{2,1,0:T(8,128)(2,1)S(1)} %collective-permute-done.1.blocks_ref, bf16[320,1280]{1,0:T(8,128)(2,1)} %get-tuple-element.43.refs_0_, ...), custom_call_target="tpu_custom_call", output_to_operand_aliasing={{0}: (2, {}), {1}: (3, {})} | custom-call | flops 1000000000 | bytes 2000000 | tf_op jit(solution)/shard_map/pallas_call | solution.py:231
  (1 shorter events, 0.0 us)
Async XLA Ops:
  2.1 10.7 %copy-start.4 = (f32[1,1280]{1,0:T(1,128)S(1)}, f32[1,1280]{1,0:T(1,128)}, u32[]{:S(2)}) copy-start(f32[1,1280]{1,0:T(1,128)} %norm_ref.1) | copy-start | bytes 15364
  2.1 10.7 %copy-start.5 = (f32[1,1280]{1,0:T(1,128)S(1)}, f32[1,1280]{1,0:T(1,128)}, u32[]{:S(2)}) copy-start(f32[1,1280]{1,0:T(1,128)} %bias_ref.1) | copy-start | bytes 15364
  2.1 10.7 %collective-permute-start = (bf16[320,1280]{1,0:T(8,128)(2,1)S(1)}, bf16[320,1280]{1,0:T(8,128)(2,1)S(1)}, u32[]{:S(2)}, u32[]{:S(2)}) collective-permute-start(bf16[320,1280]{1,0:T(8,128)(2,1)S(1)} %shard_map.212), channel_id=1, source_target_pairs={{0,16},{16,0},{1,17},{17,1},{2,18},{18,2},{3,19},{19,3},{4,20},{20... | collective-permute-start | bytes 2457608 | tf_op jit(solution)/shard_map/ppermute | solution.py:251
  12.3 19.1 %copy-start = (f32[40,320]{1,0:T(8,128)S(1)}, f32[40,320]{1,0:T(8,128)}, u32[]{:S(2)}) copy-start(f32[40,320]{1,0:T(8,128)} %refs_0_.1) | copy-start | bytes 153604
  12.3 19.1 %copy-start.1 = (f32[320,40]{0,1:T(8,128)S(1)}, f32[320,40]{0,1:T(8,128)}, u32[]{:S(2)}) copy-start(f32[320,40]{0,1:T(8,128)} %param.17) | copy-start | bytes 153604
  12.3 19.1 %copy-start.2 = (f32[40,320]{1,0:T(8,128)S(1)}, f32[40,320]{1,0:T(8,128)}, u32[]{:S(2)}) copy-start(f32[40,320]{1,0:T(8,128)} %refs_4_.1) | copy-start | bytes 153604
  12.4 19.1 %copy-start.3 = (f32[320,40]{0,1:T(8,128)S(1)}, f32[320,40]{0,1:T(8,128)}, u32[]{:S(2)}) copy-start(f32[320,40]{0,1:T(8,128)} %param.21) | copy-start | bytes 153604
  12.4 19.1 %copy-start.6 = (f32[40]{0:T(128)S(1)}, f32[40]{0:T(128)}, u32[]{:S(2)}) copy-start(f32[40]{0:T(128)} %refs_2_.1) | copy-start | bytes 484
  12.4 19.1 %copy-start.7 = (f32[40]{0:T(128)S(1)}, f32[40]{0:T(128)}, u32[]{:S(2)}) copy-start(f32[40]{0:T(128)} %refs_3_.1) | copy-start | bytes 484
  12.4 19.1 %copy-start.8 = (f32[40]{0:T(128)S(1)}, f32[40]{0:T(128)}, u32[]{:S(2)}) copy-start(f32[40]{0:T(128)} %refs_6_.1) | copy-start | bytes 484
  12.4 19.1 %copy-start.9 = (f32[40]{0:T(128)S(1)}, f32[40]{0:T(128)}, u32[]{:S(2)}) copy-start(f32[40]{0:T(128)} %refs_7_.1) | copy-start | bytes 484
  50.3 4.4 %collective-permute-start.1 = (bf16[32,104,128]{2,1,0:T(8,128)(2,1)S(1)}, bf16[32,104,128]{2,1,0:T(8,128)(2,1)S(1)}, u32[]{:S(2)}, u32[]{:S(2)}) collective-permute-start(bf16[32,104,128]{2,1,0:T(8,128)(2,1)S(1)} %all_to_all.11.blocks_ref), channel_id=1, source_target_pairs={{0,16},{16,0},{1,17},{17,1},{2,18},{18,2},{3,19},{19,3},{4,20},{20... | collective-permute-start | bytes 2555912 | tf_op jit(solution)/shard_map/ppermute | solution.py:251

commit v5 on v4

--- a/solution.py
+++ b/solution.py
@@ -8,8 +8,10 @@
 from jax.sharding import Mesh
 from jax.sharding import PartitionSpec as P
 
-DP = ("dp_0", "dp_1", "dp_2")
-CORE = "dp_2"
+DP = ("y_1", "y_0", "x_1", "x_0", "core")
+CORE = "core"
+GATHER = ("x_1", "x_0", "y_1", "y_0", "core")
+SPREAD = ("y_1", "y_0", "x_1", "core", "x_0")
 
 learn_rate = 0.1
 hold_rate = 0.7
@@ -29,6 +31,14 @@
 ROOM = pltpu.CompilerParams(vmem_limit_bytes=8 * 2**20)
 FIRST = pltpu.CompilerParams(vmem_limit_bytes=55500000)
 SECOND = pltpu.CompilerParams(vmem_limit_bytes=55000000)
+
+
+def turn(owner, path):
+    bits = {axis: owner >> (len(DP) - 1 - i) & 1 for i, axis in enumerate(DP)}
+    place = 0
+    for axis in path:
+        place = 2 * place + bits[axis]
+    return place
 
 
 def eye(rows, cols, period=None):
@@ -108,7 +118,7 @@
     for d in range(WIDTH // SHARE):
         at = d * SHARE
         rows = slice(at, at + SHARE)
-        out_ref[d] = packed(
+        out_ref[turn(d, GATHER)] = packed(
             turned[rows, :128], turned[rows, 128:256], turned[rows, 256:], line[:, at : at + 128]
         ).astype(jnp.bfloat16)
 
@@ -133,9 +143,9 @@
     params, states, (half_ref, *nexts), news = refs[:4], refs[4:8], refs[8:13], refs[13:]
     halves, lines = [], 0.0
     for c in range(2):
-        total = got_ref[c].astype(jnp.float32)
-        for i in range(1, got_ref.shape[0] // 2):
-            total += got_ref[2 * i + c].astype(jnp.float32)
+        total = got_ref[turn(c, GATHER)].astype(jnp.float32)
+        for d in range(2 + c, got_ref.shape[0], 2):
+            total += got_ref[turn(d, GATHER)].astype(jnp.float32)
         folded = total[2 * SHARE :]
         shifted = jnp.concatenate([folded[:, HALF:], folded[:, :HALF]], axis=1)
         lines += shifted[SHARE - FOLD :]
@@ -157,7 +167,7 @@
         corner = jnp.where(row == c, jnp.broadcast_to(line, (8, 128)), corner)
     halves = [packed(*half, corner).astype(jnp.bfloat16) for half in halves]
     for d in range(half_ref.shape[0]):
-        half_ref[d] = halves[d % 2]
+        half_ref[turn(d, SPREAD)] = halves[d % 2]
 
 
 def update(rate, got, params, states):
@@ -196,7 +206,7 @@
     for k in range(WIDTH // DEEP):
         while d * SHARE < (k + 1) * DEEP:
             at = d * SHARE
-            block = blocks_ref[d].astype(jnp.float32)
+            block = blocks_ref[turn(d, SPREAD)].astype(jnp.float32)
             wide[at : at + SHARE, :128] = block[:SHARE]
             wide[at : at + SHARE, 128:] = block[SHARE : 2 * SHARE]
             tail = block[2 * SHARE :]
@@ -251,8 +261,8 @@
     return lax.ppermute(x, CORE, [(0, 1), (1, 0)])
 
 
-def exchanged(x):
-    return lax.all_to_all(x, DP, 0, 0, tiled=True)
+def exchanged(x, path):
+    return lax.all_to_all(x, path, 0, 0, tiled=True)
 
 
 def body(
@@ -277,8 +287,8 @@
 
     other = swapped(pick(FIRST, 1 - core, *slopes))
     mine = pick(SECOND, core, *slopes)
-    half, *held = update(rate, exchanged(split(mine, other, slope_norm, slope_bias)), params, states)
-    mine = exchanged(half)
+    half, *held = update(rate, exchanged(split(mine, other, slope_norm, slope_bias), GATHER), params, states)
+    mine = exchanged(half, SPREAD)
     other = swapped(mine)
     lines, *begun, next_up, next_down, next_norm, next_bias, new_up, new_down, new_norm, new_bias = join(
         core, mine, held
@@ -301,7 +311,7 @@
 
 
 def solution(mesh):
-    torus = Mesh(mesh.devices.reshape(4, 4, 2, mesh.shape["tp"]), ("dp_0", "dp_1", "dp_2", "tp"))
+    torus = Mesh(mesh.devices.reshape(2, 2, 2, 2, 2, mesh.shape["tp"]), (*DP, "tp"))
     placed = (
         P(DP, None, "tp"),
         P(DP, "tp", None),

time: 56.2 us -> 55.5 us (0.988)
  blocking collectives: 36.6 us -> 34.9 us
  starting transfers between devices: 11.2 us -> 12.2 us
    all_to_all x2, blocking collectives: 36.6 us -> 34.9 us  [exchanged(): return lax.all_to_all(x, path, 0, 0, tiled=True)]
    ppermute x2, starting transfers between devices: 11.2 us -> 12.2 us  [swapped(): return lax.ppermute(x, CORE, [(0, 1), (1, 0)])]
where the time goes in v5:
time: 55.5 us; the launch traced here: 55.2 us
  blocking collectives  34.9 us (63%)
  starting transfers between devices  12.2 us (22%)
  Pallas kernels  6.15 us (11%)
  between operations  0.83 us (1%)
  local copies, waits for them, and re-layouts  0.7 us (1%)
    all_to_all x2, blocking collectives, exchanged(): return lax.all_to_all(x, path, 0, 0, tiled=True)  34.9 us
    ppermute x2, starting transfers between devices, swapped(): return lax.ppermute(x, CORE, [(0, 1), (1, 0)])  12.2 us
    pallas_call x2, Pallas kernels, pick(): pl.pallas_call(pick_kernel, in_specs=[SMEM, HBM, HBM], out_specs=VMEM, ou...  2.87 us
    pallas_call x2, Pallas kernels, join(): pl.pallas_call(functools.partial(join_kernel, len(small)), in_specs=[SMEM...  2.5 us
  transfers between devices with their start and end apart: 2, of which 1 were waited for; matrix products, arithmetic and copies ran while one was open for 1% of the time, Pallas kernels for 5%

profile of v5, /device:TPU:1, one launch (start us, length us, event | category | flops | bytes accessed | tf_op | source)
XLA Modules:
  0.0 55.2 jit_solution(3579427870241629613)
XLA Ops:
  0.6 1.4 %shard_map.212 = bf16[320,1280]{1,0:T(8,128)(2,1)S(1)} custom-call(s32[1]{0:T(128)S(6)} %sub.4.want_ref.core_ref, f32[320,1280]{1,0:T(8,128)} %bitcast.12, f32[320,1280]{1,0:T(8,128)} %bitcast.14), custom_call_target="tpu_custom_call" | custom-call | flops 1000000 | bytes 3000000 | tf_op jit(solution)/shard_map/pallas_call | solution.py:93
  2.1 0.0 copy-start.4
  2.1 0.0 copy-start.5
  2.1 8.8 %collective-permute-start = (bf16[320,1280]{1,0:T(8,128)(2,1)S(1)}, bf16[320,1280]{1,0:T(8,128)(2,1)S(1)}, u32[]{:S(2)}, u32[]{:S(2)}) collective-permute-start(bf16[320,1280]{1,0:T(8,128)(2,1)S(1)} %shard_map.212), channel_id=1, source_target_pairs={{0,16},{16,0},{1,17},{17,1},{2,18},{18,2},{3,19},{19,3},{4,20},{20... | collective-permute-start | bytes 2457608 | tf_op jit(solution)/shard_map/ppermute | solution.py:261
  10.9 1.4 %shard_map.211.mine_ref = bf16[320,1280]{1,0:T(8,128)(2,1)S(1)} custom-call(s32[1]{0:T(128)} %bitcast.want_ref.core_ref, f32[320,1280]{1,0:T(8,128)} %bitcast.13, f32[320,1280]{1,0:T(8,128)} %bitcast.15), custom_call_target="tpu_custom_call" | custom-call | flops 1000000 | bytes 3000000 | tf_op jit(solution)/shard_map/pallas_call | solution.py:93
  12.3 0.0 copy-start
  12.3 0.0 copy-start.1
  12.3 0.0 copy-start.2
  12.4 0.0 copy-start.3
  12.4 0.0 copy-start.6
  12.4 0.0 copy-start.7
  12.4 0.0 copy-start.8
  12.4 0.0 copy-start.9
  12.4 0.4 collective-permute-done.other_ref
  12.8 0.0 copy-done.4
  12.8 0.0 copy-done.5
  12.8 0.5 shard_map.213
  13.3 18.0 %all_to_all.10.got_ref = bf16[32,104,128]{2,1,0:T(8,128)(2,1)S(1)} all-to-all(bf16[32,104,128]{2,1,0:T(8,128)(2,1)S(1)} %shard_map.213), channel_id=1, replica_groups=mesh['y_1'=2,'y_0'=2,'x_1'=2,'x_0'=2,'core'=2,'tp'=16] {'x_1','x_0','y_1..., dimensions={0} | all-to-all | bytes 1703936 | tf_op jit(solution)/shard_map/all_to_all | solution.py:265
  31.4 0.0 copy-done
  31.4 0.0 copy-done.1
  31.4 0.0 copy-done.2
  31.4 0.0 copy-done.3
  31.4 0.0 copy-done.6
  31.4 0.0 copy-done.7
  31.4 0.0 copy-done.8
  31.4 0.3 shard_map.214
  31.7 16.9 %all_to_all.11.blocks_ref = bf16[32,104,128]{2,1,0:T(8,128)(2,1)S(1)} all-to-all(bf16[32,104,128]{2,1,0:T(8,128)(2,1)S(1)} %get-tuple-element.34), channel_id=1, replica_groups=mesh['y_1'=2,'y_0'=2,'x_1'=2,'x_0'=2,'core'=2,'tp'=16] {'y_1','y_0','x_1..., dimensions={0} | all-to-all | bytes 1703936 | tf_op jit(solution)/shard_map/all_to_all | solution.py:265
  48.6 3.4 %collective-permute-start.1 = (bf16[32,104,128]{2,1,0:T(8,128)(2,1)S(1)}, bf16[32,104,128]{2,1,0:T(8,128)(2,1)S(1)}, u32[]{:S(2)}, u32[]{:S(2)}) collective-permute-start(bf16[32,104,128]{2,1,0:T(8,128)(2,1)S(1)} %all_to_all.11.blocks_ref), channel_id=1, source_target_pairs={{0,16},{16,0},{1,17},{17,1},{2,18},{18,2},{3,19},{19,3},{4,20},{20... | collective-permute-start | bytes 2555912 | tf_op jit(solution)/shard_map/ppermute | solution.py:261
  52.0 1.3 %shard_map.215 = (bf16[8,1280]{1,0:T(8,128)(2,1)S(1)}, bf16[320,1280]{1,0:T(8,128)(2,1)}, bf16[320,1280]{1,0:T(8,128)(2,1)}, f32[40,320]{1,0:T(8,128)}, f32[40,3...) custom-call(s32[1]{0:T(128)} %bitcast.want_ref.core_ref, ...), custom_call_target="tpu_custom_call" | custom-call | flops 1000000000 | bytes 2000000 | tf_op jit(solution)/shard_map/pallas_call | solution.py:241
  53.3 0.6 %slice_reduce_fusion = (bf16[1280]{0:T(1024)(128)(2,1)}, bf16[1280]{0:T(1024)(128)(2,1)}) fusion(bf16[8,1280]{1,0:T(8,128)(2,1)S(1)} %get-tuple-element.47), kind=kLoop, calls=%fused_computation | loop fusion | bytes 10240 | tf_op jit(solution)/shard_map/slice | solution.py:301
  53.9 0.0 collective-permute-done.1.blocks_ref
  54.0 1.2 %shard_map.216 = (bf16[320,1280]{1,0:T(8,128)(2,1)}, bf16[320,1280]{1,0:T(8,128)(2,1)}) custom-call(s32[1]{0:T(128)S(6)} %sub.4.want_ref.core_ref, bf16[32,104,128]{2,1,0:T(8,128)(2,1)S(1)} %collective-permute-done.1.blocks_ref, bf16[320,1280]{1,0:T(8,128)(2,1)} %get-tuple-element.43.refs_0_, ...), custom_call_target="tpu_custom_call", output_to_operand_aliasing={{0}: (2, {}), {1}: (3, {})} | custom-call | flops 1000000000 | bytes 2000000 | tf_op jit(solution)/shard_map/pallas_call | solution.py:241
  (1 shorter events, 0.0 us)
Async XLA Ops:
  2.1 10.7 %copy-start.4 = (f32[1,1280]{1,0:T(1,128)S(1)}, f32[1,1280]{1,0:T(1,128)}, u32[]{:S(2)}) copy-start(f32[1,1280]{1,0:T(1,128)} %norm_ref.1) | copy-start | bytes 15364
  2.1 10.7 %copy-start.5 = (f32[1,1280]{1,0:T(1,128)S(1)}, f32[1,1280]{1,0:T(1,128)}, u32[]{:S(2)}) copy-start(f32[1,1280]{1,0:T(1,128)} %bias_ref.1) | copy-start | bytes 15364
  2.1 10.7 %collective-permute-start = (bf16[320,1280]{1,0:T(8,128)(2,1)S(1)}, bf16[320,1280]{1,0:T(8,128)(2,1)S(1)}, u32[]{:S(2)}, u32[]{:S(2)}) collective-permute-start(bf16[320,1280]{1,0:T(8,128)(2,1)S(1)} %shard_map.212), channel_id=1, source_target_pairs={{0,16},{16,0},{1,17},{17,1},{2,18},{18,2},{3,19},{19,3},{4,20},{20... | collective-permute-start | bytes 2457608 | tf_op jit(solution)/shard_map/ppermute | solution.py:261
  12.3 19.1 %copy-start = (f32[40,320]{1,0:T(8,128)S(1)}, f32[40,320]{1,0:T(8,128)}, u32[]{:S(2)}) copy-start(f32[40,320]{1,0:T(8,128)} %refs_0_.1) | copy-start | bytes 153604
  12.3 19.0 %copy-start.1 = (f32[320,40]{0,1:T(8,128)S(1)}, f32[320,40]{0,1:T(8,128)}, u32[]{:S(2)}) copy-start(f32[320,40]{0,1:T(8,128)} %param.17) | copy-start | bytes 153604
  12.3 19.0 %copy-start.2 = (f32[40,320]{1,0:T(8,128)S(1)}, f32[40,320]{1,0:T(8,128)}, u32[]{:S(2)}) copy-start(f32[40,320]{1,0:T(8,128)} %refs_4_.1) | copy-start | bytes 153604
  12.4 19.0 %copy-start.3 = (f32[320,40]{0,1:T(8,128)S(1)}, f32[320,40]{0,1:T(8,128)}, u32[]{:S(2)}) copy-start(f32[320,40]{0,1:T(8,128)} %param.21) | copy-start | bytes 153604
  12.4 19.0 %copy-start.6 = (f32[40]{0:T(128)S(1)}, f32[40]{0:T(128)}, u32[]{:S(2)}) copy-start(f32[40]{0:T(128)} %refs_2_.1) | copy-start | bytes 484
  12.4 19.0 %copy-start.7 = (f32[40]{0:T(128)S(1)}, f32[40]{0:T(128)}, u32[]{:S(2)}) copy-start(f32[40]{0:T(128)} %refs_3_.1) | copy-start | bytes 484
  12.4 19.0 %copy-start.8 = (f32[40]{0:T(128)S(1)}, f32[40]{0:T(128)}, u32[]{:S(2)}) copy-start(f32[40]{0:T(128)} %refs_6_.1) | copy-start | bytes 484
  12.4 19.0 %copy-start.9 = (f32[40]{0:T(128)S(1)}, f32[40]{0:T(128)}, u32[]{:S(2)}) copy-start(f32[40]{0:T(128)} %refs_7_.1) | copy-start | bytes 484
  48.6 5.4 %collective-permute-start.1 = (bf16[32,104,128]{2,1,0:T(8,128)(2,1)S(1)}, bf16[32,104,128]{2,1,0:T(8,128)(2,1)S(1)}, u32[]{:S(2)}, u32[]{:S(2)}) collective-permute-start(bf16[32,104,128]{2,1,0:T(8,128)(2,1)S(1)} %all_to_all.11.blocks_ref), channel_id=1, source_target_pairs={{0,16},{16,0},{1,17},{17,1},{2,18},{18,2},{3,19},{19,3},{4,20},{20... | collective-permute-start | bytes 2555912 | tf_op jit(solution)/shard_map/ppermute | solution.py:261

commit v6 on v5

--- a/solution.py
+++ b/solution.py
@@ -24,6 +24,7 @@
 HALF = 64
 DEEP = 256
 PIECES = 4
+BANDS = ((0, 128), (128, 128), (256, HALF))
 
 VMEM = pl.BlockSpec(memory_space=pltpu.VMEM)
 SMEM = pl.BlockSpec(memory_space=pltpu.SMEM)
@@ -194,30 +195,33 @@
     is_up = core_ref[0] == 0
 
     def copy(to, k):
-        lanes = pl.ds(k * DEEP, DEEP)
-        return pltpu.make_async_copy(out.at[:, lanes], to.at[:, lanes], sems.at[small + k])
+        rows = pl.ds(*BANDS[k])
+        return pltpu.make_async_copy(out.at[rows], to.at[rows], sems.at[small + k])
 
     low = low_lanes(FOLD)
     upper = SHARE - FOLD
     pieces = []
-    one = eye(DEEP, DEEP)
+    one = eye(128, 128)
     folded = eye(HALF, 128, HALF)
-    d = 0
-    for k in range(WIDTH // DEEP):
-        while d * SHARE < (k + 1) * DEEP:
+    for k, (first, many) in enumerate(BANDS):
+        for d in range(WIDTH // SHARE):
             at = d * SHARE
-            block = blocks_ref[turn(d, SPREAD)].astype(jnp.float32)
-            wide[at : at + SHARE, :128] = block[:SHARE]
-            wide[at : at + SHARE, 128:] = block[SHARE : 2 * SHARE]
-            tail = block[2 * SHARE :]
-            tails[at : at + FOLD] = jnp.where(low, tail, 0.0)
-            tails[at + FOLD : at + SHARE] = jnp.where(low[:upper], 0.0, tail[:upper])
-            if small:
-                pieces.append(tail[upper:, HALF : HALF + SHARE])
-            d += 1
-        lanes = slice(k * DEEP, (k + 1) * DEEP)
-        out[:256, lanes] = times_transposed(one, wide[lanes].astype(jnp.bfloat16)).astype(jnp.bfloat16)
-        out[256:, lanes] = times_transposed(folded, tails[lanes].astype(jnp.bfloat16)).astype(jnp.bfloat16)
+            if many == HALF:
+                tail = blocks_ref[turn(d, SPREAD), 2 * SHARE :].astype(jnp.float32)
+                tails[at : at + FOLD] = jnp.where(low, tail, 0.0)
+                tails[at + FOLD : at + SHARE] = jnp.where(low[:upper], 0.0, tail[:upper])
+                if small:
+                    pieces.append(tail[upper:, HALF : HALF + SHARE])
+            else:
+                rows = slice(first // 128 * SHARE, (first // 128 + 1) * SHARE)
+                wide[at : at + SHARE, first : first + 128] = blocks_ref[turn(d, SPREAD), rows].astype(jnp.float32)
+        for n in range(WIDTH // DEEP):
+            lanes = slice(n * DEEP, (n + 1) * DEEP)
+            if many == HALF:
+                band = times_transposed(folded, tails[lanes].astype(jnp.bfloat16))
+            else:
+                band = times_transposed(one, wide[lanes, first : first + 128].astype(jnp.bfloat16))
+            out[first : first + many, lanes] = band.astype(jnp.bfloat16)
 
         @pl.when(is_up)
         def _():
@@ -231,7 +235,7 @@
         lines_ref[...] = jnp.concatenate(pieces, axis=1).astype(jnp.bfloat16)
     for write in writes:
         write.wait()
-    for k in range(WIDTH // DEEP):
+    for k in range(len(BANDS)):
         copy(up_ref, k).wait()
 
 
@@ -250,7 +254,7 @@
             pltpu.VMEM((WIDTH, 256), jnp.float32),
             pltpu.VMEM((WIDTH, 128), jnp.float32),
             pltpu.VMEM((COLS, WIDTH), jnp.bfloat16),
-            pltpu.SemaphoreType.DMA((len(small) + WIDTH // DEEP,)),
+            pltpu.SemaphoreType.DMA((len(small) + len(BANDS),)),
         ],
         compiler_params=ROOM,
         cost_estimate=pl.CostEstimate(flops=10**9, bytes_accessed=2 * 10**6, transcendentals=0),

time: 55.5 us -> 55.4 us (level)
  transfers between devices with their start and end apart: 2 -> 2, of which waited for: 1 -> 2; matrix products, arithmetic and copies ran while one was open for 1% -> 1% of each run, Pallas kernels for 5% -> 5%
where the time goes in v6:
time: 55.4 us; the launch traced here: 55.1 us
  blocking collectives  34.9 us (63%)
  starting transfers between devices  12.2 us (22%)
  Pallas kernels  6.07 us (11%)
  between operations  0.83 us (1%)
  local copies, waits for them, and re-layouts  0.7 us (1%)
    all_to_all x2, blocking collectives, exchanged(): return lax.all_to_all(x, path, 0, 0, tiled=True)  34.9 us
    ppermute x2, starting transfers between devices, swapped(): return lax.ppermute(x, CORE, [(0, 1), (1, 0)])  12.2 us
    pallas_call x2, Pallas kernels, pick(): pl.pallas_call(pick_kernel, in_specs=[SMEM, HBM, HBM], out_specs=VMEM, ou...  2.87 us
    pallas_call x2, Pallas kernels, join(): pl.pallas_call(functools.partial(join_kernel, len(small)), in_specs=[SMEM...  2.43 us
  transfers between devices with their start and end apart: 2, of which 2 were waited for; matrix products, arithmetic and copies ran while one was open for 1% of the time, Pallas kernels for 5%

profile of v6, /device:TPU:1, one launch (start us, length us, event | category | flops | bytes accessed | tf_op | source)
XLA Modules:
  0.0 55.1 jit_solution(12530883971937265718)
XLA Ops:
  0.6 1.4 %shard_map.212 = bf16[320,1280]{1,0:T(8,128)(2,1)S(1)} custom-call(s32[1]{0:T(128)S(6)} %sub.4.want_ref.core_ref, f32[320,1280]{1,0:T(8,128)} %bitcast.12, f32[320,1280]{1,0:T(8,128)} %bitcast.14), custom_call_target="tpu_custom_call" | custom-call | flops 1000000 | bytes 3000000 | tf_op jit(solution)/shard_map/pallas_call | solution.py:94
  2.1 0.0 copy-start.4
  2.1 0.0 copy-start.5
  2.1 8.8 %collective-permute-start = (bf16[320,1280]{1,0:T(8,128)(2,1)S(1)}, bf16[320,1280]{1,0:T(8,128)(2,1)S(1)}, u32[]{:S(2)}, u32[]{:S(2)}) collective-permute-start(bf16[320,1280]{1,0:T(8,128)(2,1)S(1)} %shard_map.212), channel_id=1, source_target_pairs={{0,16},{16,0},{1,17},{17,1},{2,18},{18,2},{3,19},{19,3},{4,20},{20... | collective-permute-start | bytes 2457608 | tf_op jit(solution)/shard_map/ppermute | solution.py:265
  10.9 1.4 %shard_map.211.mine_ref = bf16[320,1280]{1,0:T(8,128)(2,1)S(1)} custom-call(s32[1]{0:T(128)} %bitcast.want_ref.core_ref, f32[320,1280]{1,0:T(8,128)} %bitcast.13, f32[320,1280]{1,0:T(8,128)} %bitcast.15), custom_call_target="tpu_custom_call" | custom-call | flops 1000000 | bytes 3000000 | tf_op jit(solution)/shard_map/pallas_call | solution.py:94
  12.3 0.0 copy-start
  12.3 0.0 copy-start.1
  12.3 0.0 copy-start.2
  12.4 0.0 copy-start.3
  12.4 0.0 copy-start.6
  12.4 0.0 copy-start.7
  12.4 0.0 copy-start.8
  12.4 0.0 copy-start.9
  12.4 0.4 collective-permute-done.other_ref
  12.8 0.0 copy-done.4
  12.8 0.0 copy-done.5
  12.8 0.5 shard_map.213
  13.3 18.0 %all_to_all.10.got_ref = bf16[32,104,128]{2,1,0:T(8,128)(2,1)S(1)} all-to-all(bf16[32,104,128]{2,1,0:T(8,128)(2,1)S(1)} %shard_map.213), channel_id=1, replica_groups=mesh['y_1'=2,'y_0'=2,'x_1'=2,'x_0'=2,'core'=2,'tp'=16] {'x_1','x_0','y_1..., dimensions={0} | all-to-all | bytes 1703936 | tf_op jit(solution)/shard_map/all_to_all | solution.py:269
  31.4 0.0 copy-done
  31.4 0.0 copy-done.1
  31.4 0.0 copy-done.3
  31.4 0.0 copy-done.6
  31.4 0.0 copy-done.7
  31.4 0.0 copy-done.8
  31.4 0.0 copy-done.9
  31.4 0.3 shard_map.214
  31.7 16.9 %all_to_all.11.blocks_ref = bf16[32,104,128]{2,1,0:T(8,128)(2,1)S(1)} all-to-all(bf16[32,104,128]{2,1,0:T(8,128)(2,1)S(1)} %get-tuple-element.34), channel_id=1, replica_groups=mesh['y_1'=2,'y_0'=2,'x_1'=2,'x_0'=2,'core'=2,'tp'=16] {'y_1','y_0','x_1..., dimensions={0} | all-to-all | bytes 1703936 | tf_op jit(solution)/shard_map/all_to_all | solution.py:269
  48.6 3.4 %collective-permute-start.1 = (bf16[32,104,128]{2,1,0:T(8,128)(2,1)S(1)}, bf16[32,104,128]{2,1,0:T(8,128)(2,1)S(1)}, u32[]{:S(2)}, u32[]{:S(2)}) collective-permute-start(bf16[32,104,128]{2,1,0:T(8,128)(2,1)S(1)} %all_to_all.11.blocks_ref), channel_id=1, source_target_pairs={{0,16},{16,0},{1,17},{17,1},{2,18},{18,2},{3,19},{19,3},{4,20},{20... | collective-permute-start | bytes 2555912 | tf_op jit(solution)/shard_map/ppermute | solution.py:265
  52.0 1.3 %shard_map.215 = (bf16[8,1280]{1,0:T(8,128)(2,1)S(1)}, bf16[320,1280]{1,0:T(8,128)(2,1)}, bf16[320,1280]{1,0:T(8,128)(2,1)}, f32[40,320]{1,0:T(8,128)}, f32[40,3...) custom-call(s32[1]{0:T(128)} %bitcast.want_ref.core_ref, ...), custom_call_target="tpu_custom_call" | custom-call | flops 1000000000 | bytes 2000000 | tf_op jit(solution)/shard_map/pallas_call | solution.py:245
  53.2 0.6 %slice_reduce_fusion = (bf16[1280]{0:T(1024)(128)(2,1)}, bf16[1280]{0:T(1024)(128)(2,1)}) fusion(bf16[8,1280]{1,0:T(8,128)(2,1)S(1)} %get-tuple-element.47), kind=kLoop, calls=%fused_computation | loop fusion | bytes 10240 | tf_op jit(solution)/shard_map/slice | solution.py:305
  53.9 0.1 collective-permute-done.1.blocks_ref
  54.0 1.2 %shard_map.216 = (bf16[320,1280]{1,0:T(8,128)(2,1)}, bf16[320,1280]{1,0:T(8,128)(2,1)}) custom-call(s32[1]{0:T(128)S(6)} %sub.4.want_ref.core_ref, bf16[32,104,128]{2,1,0:T(8,128)(2,1)S(1)} %collective-permute-done.1.blocks_ref, bf16[320,1280]{1,0:T(8,128)(2,1)} %get-tuple-element.43.refs_0_, ...), custom_call_target="tpu_custom_call", output_to_operand_aliasing={{0}: (2, {}), {1}: (3, {})} | custom-call | flops 1000000000 | bytes 2000000 | tf_op jit(solution)/shard_map/pallas_call | solution.py:245
  (1 shorter events, 0.0 us)
Async XLA Ops:
  2.1 10.7 %copy-start.4 = (f32[1,1280]{1,0:T(1,128)S(1)}, f32[1,1280]{1,0:T(1,128)}, u32[]{:S(2)}) copy-start(f32[1,1280]{1,0:T(1,128)} %norm_ref.1) | copy-start | bytes 15364
  2.1 10.7 %copy-start.5 = (f32[1,1280]{1,0:T(1,128)S(1)}, f32[1,1280]{1,0:T(1,128)}, u32[]{:S(2)}) copy-start(f32[1,1280]{1,0:T(1,128)} %bias_ref.1) | copy-start | bytes 15364
  2.1 10.7 %collective-permute-start = (bf16[320,1280]{1,0:T(8,128)(2,1)S(1)}, bf16[320,1280]{1,0:T(8,128)(2,1)S(1)}, u32[]{:S(2)}, u32[]{:S(2)}) collective-permute-start(bf16[320,1280]{1,0:T(8,128)(2,1)S(1)} %shard_map.212), channel_id=1, source_target_pairs={{0,16},{16,0},{1,17},{17,1},{2,18},{18,2},{3,19},{19,3},{4,20},{20... | collective-permute-start | bytes 2457608 | tf_op jit(solution)/shard_map/ppermute | solution.py:265
  12.3 19.1 %copy-start = (f32[40,320]{1,0:T(8,128)S(1)}, f32[40,320]{1,0:T(8,128)}, u32[]{:S(2)}) copy-start(f32[40,320]{1,0:T(8,128)} %refs_0_.1) | copy-start | bytes 153604
  12.3 19.0 %copy-start.1 = (f32[320,40]{0,1:T(8,128)S(1)}, f32[320,40]{0,1:T(8,128)}, u32[]{:S(2)}) copy-start(f32[320,40]{0,1:T(8,128)} %param.17) | copy-start | bytes 153604
  12.3 19.0 %copy-start.2 = (f32[40,320]{1,0:T(8,128)S(1)}, f32[40,320]{1,0:T(8,128)}, u32[]{:S(2)}) copy-start(f32[40,320]{1,0:T(8,128)} %refs_4_.1) | copy-start | bytes 153604
  12.4 19.0 %copy-start.3 = (f32[320,40]{0,1:T(8,128)S(1)}, f32[320,40]{0,1:T(8,128)}, u32[]{:S(2)}) copy-start(f32[320,40]{0,1:T(8,128)} %param.21) | copy-start | bytes 153604
  12.4 19.0 %copy-start.6 = (f32[40]{0:T(128)S(1)}, f32[40]{0:T(128)}, u32[]{:S(2)}) copy-start(f32[40]{0:T(128)} %refs_2_.1) | copy-start | bytes 484
  12.4 19.0 %copy-start.7 = (f32[40]{0:T(128)S(1)}, f32[40]{0:T(128)}, u32[]{:S(2)}) copy-start(f32[40]{0:T(128)} %refs_3_.1) | copy-start | bytes 484
  12.4 19.0 %copy-start.8 = (f32[40]{0:T(128)S(1)}, f32[40]{0:T(128)}, u32[]{:S(2)}) copy-start(f32[40]{0:T(128)} %refs_6_.1) | copy-start | bytes 484
  12.4 19.0 %copy-start.9 = (f32[40]{0:T(128)S(1)}, f32[40]{0:T(128)}, u32[]{:S(2)}) copy-start(f32[40]{0:T(128)} %refs_7_.1) | copy-start | bytes 484
  48.6 5.4 %collective-permute-start.1 = (bf16[32,104,128]{2,1,0:T(8,128)(2,1)S(1)}, bf16[32,104,128]{2,1,0:T(8,128)(2,1)S(1)}, u32[]{:S(2)}, u32[]{:S(2)}) collective-permute-start(bf16[32,104,128]{2,1,0:T(8,128)(2,1)S(1)} %all_to_all.11.blocks_ref), channel_id=1, source_target_pairs={{0,16},{16,0},{1,17},{17,1},{2,18},{18,2},{3,19},{19,3},{4,20},{20... | collective-permute-start | bytes 2555912 | tf_op jit(solution)/shard_map/ppermute | solution.py:265
